TPU v7x, 256 devices: a 4x2x16 block of a 4x16x16 slice. The times are simulated.
256 devices in a mesh: grp: 2 (over y), slab: 16 (over z), blk: 4 (over x), sub: 2 (over core).
Axes of the slice: x: 4, y: 2, z: 16, core: 2. Of those that a mesh axis runs over, the one named last changes fastest.
The devices are a block of a 4x16x16 slice.
Arguments:
- cell_x: int32 [65536], P(('grp', 'slab', 'blk', 'sub')), parts along dimension 0, may hold values from 0 to 63
- cell_y: int32 [65536], P(('grp', 'slab', 'blk', 'sub')), parts along dimension 0, may hold values from 0 to 127
- cell_z: int32 [65536], P(('grp', 'slab', 'blk', 'sub')), parts along dimension 0, may hold values from 0 to 127
- offsets: float32 [3, 65536], P(None, ('grp', 'slab', 'blk', 'sub')), parts along dimension 1, may hold values from 0 to 1
- charge: float32 [65536], P(('grp', 'slab', 'blk', 'sub')), parts along dimension 0, may hold values from -4 to 4
- block_count: int32 [256], P(('grp', 'slab', 'blk', 'sub')), parts along dimension 0, may hold values from 0 to 256, as said below
- level_amplitude: float32 [4], replicated, may hold values from 0.5 to 2
- density: float32 [512, 256, 256], P(('grp', 'slab'), 'blk', 'sub'), parts along dimension 0, may hold values from 0.3 to 8.2
Outputs:
- field: float32 [512, 256, 256], P(('grp', 'slab'), 'blk', 'sub'), parts along dimension 0
- energy: float32 [2], P('grp'), parts along dimension 0
There are 2 independent parts, one for each index of `grp`. A program takes and returns all parts, laid end to end along the dimension named above; an argument that names none is the same for every part. Nothing has to cross between parts.
Inputs may be any that keep to these rules, and one draw needn't show every extreme that they name: `block_count`: within the 1 block of each device, blocks with a nonzero count come before blocks with count 0; some device has every block full.
All inputs are finite; a program needn't handle non-finite values.
Results may differ from a plain program's by a relative error of at most 0.0021.
Values sent between devices are 32-bit elements; how exact they have to be, the bound alone decides.
A program may use at most 64 MiB of HBM per device.

v0:
```python
import functools

import jax
import jax.numpy as jnp
from jax import lax
from jax.sharding import PartitionSpec as P

G0X = 64
G0Y = 128
G0Z = 128
FINE_X = 256
FINE_Y = 256
FINE_Z = 256
BQ = 256


spread_width = 1.25


def rows_first(arrays, axis, dims):
    turned = [jnp.moveaxis(a, dim, 0) for a, dim in zip(arrays, dims)]
    both = jnp.concatenate([t.reshape(len(t), -1) for t in turned], axis=1)
    out, at, gathered = (lax.all_gather(both, axis, axis=0, tiled=True), 0, [])
    for t, dim in zip(turned, dims):
        share = out[:, at : at + t[0].size].reshape(-1, *t.shape[1:])
        gathered.append(jnp.moveaxis(share, 0, dim))
        at += t[0].size
    return tuple(gathered)


def over_pieces(value, axis):
    return lax.all_gather(value, axis).sum(0)


def passed_along(value, axis, by):
    peers = lax.axis_size(axis)
    return lax.ppermute(value, axis, [(i, (i + by) % peers) for i in range(peers)])


def by_axis(value, axes):
    return functools.reduce(lax.psum, axes, value)


def axis_weights(shifts, base, coarse):
    position = shifts * (coarse / base)
    nodes = jnp.arange(coarse, dtype=jnp.float32)
    distance = nodes[None, :] - position[:, None]
    distance = distance - coarse * jnp.floor(distance / coarse + 0.5)
    return jnp.exp(-0.5 * (distance / spread_width) ** 2)


def placed_weights(placed, base, coarse, first, count):
    position = placed * (coarse / base)
    nodes = first.astype(jnp.float32) + jnp.arange(count, dtype=jnp.float32)
    distance = nodes[None, :] - position[:, None]
    distance = distance - coarse * jnp.floor(distance / coarse + 0.5)
    return jnp.exp(-0.5 * (distance / spread_width) ** 2)


def level_dims():
    return [
        (G0X * (4 - factor) // 4, G0Y * (4 - factor) // 4, G0Z * (4 - factor) // 4)
        for factor in range(4)
    ]


def spread_slab(totals, pieces, slab_index, slab_count):
    weighted, placed_x, placed_y, placed_z = pieces
    result = []
    for total, (dim_x, dim_y, dim_z) in zip(totals, level_dims()):
        slab_rows = dim_x // slab_count
        along_x = placed_weights(placed_x, G0X, dim_x, slab_index * slab_rows, slab_rows)
        along_y = axis_weights(placed_y, G0Y, dim_y)
        along_z = axis_weights(placed_z, G0Z, dim_z)
        planes = (
            ((weighted[:, None] * along_x)[:, :, None] * along_y[:, None, :])
            .reshape(weighted.shape[0], slab_rows * dim_y)
            .astype(jnp.bfloat16)
        )
        result.append(
            total
            + lax.dot_general(
                planes,
                along_z.astype(jnp.bfloat16),
                (((0,), (0,)), ((), ())),
                preferred_element_type=jnp.float32,
            )
        )
    return tuple(result)


def hat_matrix(fine, coarse, first_row, rows):
    fine_rows = first_row + jnp.arange(rows, dtype=jnp.int32)
    nodes = jnp.arange(coarse, dtype=jnp.int32)
    period = coarse * fine
    moved = (nodes[None, :] * fine - fine_rows[:, None] * coarse) % period
    moved = jnp.where(moved * 2 >= period, moved - period, moved)
    distance = moved.astype(jnp.float32) / fine
    return jnp.maximum(0.0, 1.0 - jnp.abs(distance))


def local_hat(fine_rows, coarse_cols, coarse):
    row_ids = jnp.arange(fine_rows, dtype=jnp.int32)
    col_ids = jnp.arange(coarse_cols, dtype=jnp.int32)
    moved = col_ids[None, :] * FINE_X - row_ids[:, None] * coarse
    distance = moved.astype(jnp.float32) / FINE_X
    return jnp.maximum(0.0, 1.0 - jnp.abs(distance))


def interpolate(mat_x, mat_y, mat_z, cube):
    highest = lax.Precision.HIGHEST
    first = jnp.einsum("ax,xyz->ayz", mat_x, cube, precision=highest)
    second = jnp.einsum("by,ayz->abz", mat_y, first, precision=highest)
    return jnp.einsum("cz,abz->abc", mat_z, second, precision=highest)


def on_device(cell_x, cell_y, cell_z, offsets, charge, block_count, level_amplitude, density):
    blocks = block_count.shape[0]
    live = (jnp.arange(BQ, dtype=jnp.int32)[None, :] < block_count[:, None]).astype(jnp.float32)
    weighted = charge.reshape(blocks, BQ) * live
    slab_count = lax.axis_size("slab")
    slab_index = lax.axis_index("slab")
    placed_x = cell_x.astype(jnp.float32) + offsets[0]
    placed_y = cell_y.astype(jnp.float32) + offsets[1]
    placed_z = cell_z.astype(jnp.float32) + offsets[2]
    flat_weighted = weighted.reshape(-1)
    begin = tuple(
        (
            jnp.zeros((dim_x // slab_count * dim_y, dim_z), jnp.float32)
            for dim_x, dim_y, dim_z in level_dims()
        )
    )
    totals = begin
    pieces = rows_first((flat_weighted, placed_x, placed_y, placed_z), "slab", (0, 0, 0, 0))
    spread_rows = pieces[0].shape[0]
    full = spread_rows // BQ

    def one_block(number, carried):
        block = tuple((lax.dynamic_slice_in_dim(array, number * BQ, BQ) for array in pieces))
        return spread_slab(carried, block, slab_index, slab_count)

    totals = lax.fori_loop(0, full, one_block, totals)
    summed = jax.tree.map(lambda part: over_pieces(part, ("blk", "sub")), totals)
    slabs = tuple(
        (
            rows.reshape(dim_x // slab_count, dim_y, dim_z)
            for rows, (dim_x, dim_y, dim_z) in zip(summed, level_dims())
        )
    )
    firsts = tuple((piece[0:1] for piece in slabs))
    after = passed_along(firsts, "slab", -1)
    rows_x, rows_y, rows_z = density.shape
    blk_start = lax.axis_index("blk") * rows_y
    sub_start = lax.axis_index("sub") * rows_z
    field = jnp.zeros((rows_x, rows_y, rows_z), jnp.float32)
    for factor, (dim_x, dim_y, dim_z) in enumerate(level_dims()):
        extended = jnp.concatenate([slabs[factor], after[factor]], axis=0)
        mat_x = local_hat(rows_x, dim_x // slab_count + 1, dim_x)
        mat_y = hat_matrix(FINE_Y, dim_y, blk_start, rows_y)
        mat_z = hat_matrix(FINE_Z, dim_z, sub_start, rows_z)
        field = field + level_amplitude[factor] * interpolate(mat_x, mat_y, mat_z, extended)
    total = by_axis(jnp.sum(density * field), ("slab", "blk", "sub"))
    energy = (total / (FINE_X * FINE_Y * FINE_Z)).reshape(1)
    return (field, energy)


def solution(mesh):
    in_specs = (
        P(("grp", "slab", "blk", "sub")),
        P(("grp", "slab", "blk", "sub")),
        P(("grp", "slab", "blk", "sub")),
        P(None, ("grp", "slab", "blk", "sub")),
        P(("grp", "slab", "blk", "sub")),
        P(("grp", "slab", "blk", "sub")),
        P(),
        P(("grp", "slab"), "blk", "sub"),
    )
    out_specs = (P(("grp", "slab"), "blk", "sub"), P("grp"))
    return jax.shard_map(
        on_device, mesh=mesh, in_specs=in_specs, out_specs=out_specs, check_vma=False
    )
```

profile of v0, /device:TPU:33, one launch (start us, length us, event | category | flops | bytes accessed | tf_op | source)
XLA Modules:
  0.0 214.6 jit_solution(13088567531267280203)
XLA Ops:
  7.3 0.8 fusion.396
  8.7 0.7 convert_add_fusion.2
  11.5 42.4 %all_gather.27 = f32[4096,4]{0,1:T(4,128)S(1)} all-gather(f32[256,4]{0,1:T(4,128)S(1)} %pad_maximum_fusion), channel_id=1, replica_groups=mesh['grp'=2,'slab'=16,'blk'=4,'sub'=2] {'slab'}, dimensions={0}, use_global_device_ids=true | all-gather | bytes 69632 | tf_op jit(solution)/shard_map/all_gather | solution.py:23
  54.0 35.3 %while.22 = (s32[]{:T(128)}, f32[512,128]{1,0:T(8,128)S(1)}, f32[288,96]{1,0:T(8,128)S(1)}, f32[128,64]{0,1:T(8,128)S(1)}, f32[32,32]{1,0:T(8,128)S(1)}, /*index...) while((s32[]{:T(128)}, f32[512,128]{1,0:T(8,128)S(1)}, ...), condition=%wide.region_1.0_spmd.clone, body=%wide.region_0.0_spmd.clone.sunk | while | flops 54709520 | bytes 2422072 | solution.py:142
  89.3 0.7 copy-done.1
  90.1 23.4 %all-gather.1 = f32[2304,96]{1,0:T(8,128)S(1)} all-gather(f32[288,96]{1,0:T(8,128)S(1)} %get-tuple-element.257), channel_id=3, replica_groups=mesh['grp'=2,'slab'=16,'blk'=4,'sub'=2] {'blk','sub'}, dimensions={0}, use_global_device_ids=true | all-gather | bytes 995328 | tf_op jit(solution)/shard_map/all_gather | solution.py:32
  113.8 13.0 %all-gather.3 = f32[256,32]{1,0:T(8,128)S(1)} all-gather(f32[32,32]{1,0:T(8,128)S(1)} %get-tuple-element.259), channel_id=5, replica_groups=mesh['grp'=2,'slab'=16,'blk'=4,'sub'=2] {'blk','sub'}, dimensions={0}, use_global_device_ids=true | all-gather | bytes 36864 | tf_op jit(solution)/shard_map/all_gather | solution.py:32
  126.9 13.1 %all-gather.2 = f32[1024,64]{0,1:T(8,128)S(1)} all-gather(f32[128,64]{0,1:T(8,128)S(1)} %get-tuple-element.258), channel_id=4, replica_groups=mesh['grp'=2,'slab'=16,'blk'=4,'sub'=2] {'blk','sub'}, dimensions={0}, use_global_device_ids=true | all-gather | bytes 294912 | tf_op jit(solution)/shard_map/all_gather | solution.py:32
  142.8 1.7 convolution_multiply_fusion
  144.4 0.7 fusion.87
  145.2 1.1 convolution_bitcast_fusion
  146.2 1.0 fusion.83
  147.2 1.7 reduce_sum.45
  149.0 1.2 collective-permute-start
  150.1 0.9 convolution_bitcast_fusion.1
  151.2 1.8 collective-permute-done
  153.1 1.2 fusion.77
  154.2 1.0 convolution_bitcast_fusion.2
  155.3 1.3 convolution_multiply_fusion.3
  156.6 1.3 fusion.74
  157.9 3.1 %multiply_reduce_fusion = (f32[]{:T(128)}, f32[16,64,128]{2,1,0:T(8,128)}) fusion(f32[16,64,128]{2,1,0:T(8,128)S(1)} %copy-done, f32[16,64,128]{2,1,0:T(8,128)S(1)} %convolution_multiply_fusion, f32[16,64,128]{2,1,0:T(8,128)S(1)} %fusion.74, f32[16,64,64]{1,2,0:T(8,128)S(1)} %convolution_bitcast_fusion, s32[128]{0:T(128)S(1)} %fusion.309, ...), kind=kOutput, calls=%fused_computation.123 | convolution fusion | flops 101490688 | bytes 2360072 | tf_op jit(solution)/shard_map/cz,abz->abc/dot_general | solution.py:114
  161.0 23.5 %psum.21 = f32[]{:T(128)} all-reduce(f32[]{:T(128)} %get-tuple-element.354), channel_id=1, replica_groups=mesh['grp'=2,'slab'=16,'blk'=4,'sub'=2] {'slab'}, use_global_device_ids=true, to_apply=%region_7.8 | all-reduce | flops 1 | bytes 8 | tf_op jit(solution)/shard_map/psum | solution.py:41
  184.5 8.1 %psum.22 = f32[]{:T(128)} all-reduce(f32[]{:T(128)} %psum.21), channel_id=1, replica_groups=mesh['grp'=2,'slab'=16,'blk'=4,'sub'=2] {'blk'}, use_global_device_ids=true, to_apply=%region_8.9 | all-reduce | flops 1 | bytes 8 | tf_op jit(solution)/shard_map/psum | solution.py:41
  192.6 13.3 %psum.23 = f32[]{:T(128)} all-reduce(f32[]{:T(128)} %psum.22), channel_id=1, replica_groups=mesh['grp'=2,'slab'=16,'blk'=4,'sub'=2] {'sub'}, use_global_device_ids=true, to_apply=%region_9.10 | all-reduce | flops 1 | bytes 8 | tf_op jit(solution)/shard_map/psum | solution.py:41
  (406 shorter events, 39.1 us)
Async XLA Ops:
  7.2 140.1 %all-gather.6.cloned.1.call-start = ((), (), s32[]{:S(2)}) async-start(), calls=%async_computation | async-start | bytes 2359296 | tf_op jit(solution)/shard_map/all_gather | solution.py:32
  89.3 0.7 copy-start.1
  90.1 50.5 %copy-start.2 = (f32[4]{0:T(128)S(1)}, f32[4]{0:T(128)}, u32[]{:S(2)}) copy-start(f32[4]{0:T(128)} %param.16) | copy-start | bytes 52
  113.6 32.6 %collective-permute-start.1 = (f32[1,96,96]{2,0,1:T(1,128)S(1)}, f32[1,96,96]{2,0,1:T(1,128)S(1)}, u32[]{:S(2)}, u32[]{:S(2)}) collective-permute-start(f32[1,96,96]{2,0,1:T(1,128)S(1)} %bitcast.118), channel_id=1, source_target_pairs={{0,120},{8,0},{16,8},{24,16},{32,24},{40,32},{48,40},{56,48},{64,5... | collective-permute-start | bytes 110600 | tf_op jit(solution)/shard_map/ppermute | solution.py:37
  126.7 14.8 %collective-permute-start.3 = (f32[1,32,32]{2,0,1:T(1,128)S(1)}, f32[1,32,32]{2,0,1:T(1,128)S(1)}, u32[]{:S(2)}, u32[]{:S(2)}) collective-permute-start(f32[1,32,32]{2,0,1:T(1,128)S(1)} %bitcast.115), channel_id=1, source_target_pairs={{0,120},{8,0},{16,8},{24,16},{32,24},{40,32},{48,40},{56,48},{64,5... | collective-permute-start | bytes 12296 | tf_op jit(solution)/shard_map/ppermute | solution.py:37
  140.2 4.3 %collective-permute-start.2 = (f32[1,64,64]{2,0,1:T(1,128)S(1)}, f32[1,64,64]{2,0,1:T(1,128)S(1)}, u32[]{:S(2)}, u32[]{:S(2)}) collective-permute-start(f32[1,64,64]{2,0,1:T(1,128)S(1)} %bitcast.119), channel_id=1, source_target_pairs={{0,120},{8,0},{16,8},{24,16},{32,24},{40,32},{48,40},{56,48},{64,5... | collective-permute-start | bytes 49160 | tf_op jit(solution)/shard_map/ppermute | solution.py:37
  149.0 4.1 %collective-permute-start = (f32[1,128,128]{2,0,1:T(1,128)S(1)}, f32[1,128,128]{2,0,1:T(1,128)S(1)}, u32[]{:S(2)}, u32[]{:S(2)}) collective-permute-start(f32[1,128,128]{2,0,1:T(1,128)S(1)} %bitcast.117), channel_id=1, source_target_pairs={{0,120},{8,0},{16,8},{24,16},{32,24},{40,32},{48,40},{56,48},{64,5... | collective-permute-start | bytes 196616 | tf_op jit(solution)/shard_map/ppermute | solution.py:37
  154.2 3.6 %copy-start = (f32[16,64,128]{2,1,0:T(8,128)S(1)}, f32[16,64,128]{2,1,0:T(8,128)}, u32[]{:S(2)}) copy-start(f32[16,64,128]{2,1,0:T(8,128)} %param.17) | copy-start | bytes 1572868
Sparse Core Ops, SparseCore 0:
  90.2 32.4 all-gather.5
where the time goes:
time: 215 us
  blocking collectives  137 us (64%)
  matrix products  28.8 us (13%)
  other arithmetic  21.5 us (10%)
  between operations  16.9 us (8%)
  local copies, waits for them, and re-layouts  5.18 us (2%)
    all_gather x3, blocking collectives, over_pieces(): return lax.all_gather(value, axis).sum(0)  49.4 us
    psum x3, blocking collectives, by_axis(): return functools.reduce(lax.psum, axes, value)  44.9 us
    all_gather x1, blocking collectives, rows_first(): out, at, gathered = (lax.all_gather(both, axis, axis=0, tiled=True), 0, [])  42.4 us
    dot_general x64, matrix products, spread_slab(): lax.dot_general(planes, along_z.astype(jnp.bfloat16), (((0,), (0,)), ((),...  14.4 us
    dot_general x4, matrix products, interpolate(): return jnp.einsum('cz,abz->abc', mat_z, second, precision=highest)  7.4 us
    convert_element_type x48, other arithmetic, spread_slab(): planes = ((weighted[:, None] * along_x)[:, :, None] * along_y[:, None, :]...  5.89 us
    mul x64, other arithmetic, spread_slab(): weighted[:, None] * along_x  5.47 us
  transfers between devices with their start and end apart: 5, of which 1 were waited for; matrix products, arithmetic and copies ran while one was open for 4% of the time, Pallas kernels for 0%

commit v1 on v0

v1 whole, which is shorter than its diff:
```python
import functools

import jax
import jax.numpy as jnp
import numpy as np
from jax import lax
from jax.experimental import pallas as pl
from jax.experimental.pallas import tpu as pltpu
from jax.sharding import PartitionSpec as P

G0X = 64
G0Y = 128
G0Z = 128
FINE_X = 256
FINE_Y = 256
FINE_Z = 256
BQ = 256
LEVELS = 4
LANES = 128
HALO = 16
spread_width = 1.25
MESH = pl.DeviceIdType.MESH


def coarse_cells(base, level):
    return base * (4 - level) // 4


class Plan:
    def __init__(self, slabs, cols, rows_x, rows_y, rows_z):
        self.slabs, self.cols = slabs, cols
        self.rows = (rows_x, rows_y, rows_z)
        self.gx = [coarse_cells(G0X, l) for l in range(LEVELS)]
        self.gy = [coarse_cells(G0Y, l) for l in range(LEVELS)]
        self.gz = [coarse_cells(G0Z, l) for l in range(LEVELS)]
        self.nx = [g // slabs + 1 for g in self.gx]
        self.ny = [g // cols for g in self.gy]
        self.main = [a * b for a, b in zip(self.nx, self.ny)]
        self.block = [m + HALO for m in self.main]
        self.start = [sum(self.block[:l]) for l in range(LEVELS)]
        self.total = sum(self.block)
        self.xrow = [sum(self.nx[:l]) for l in range(LEVELS)]
        self.yrow = [sum(self.ny[:l]) for l in range(LEVELS)]
        self.zrow = [sum(self.gz[:l]) for l in range(LEVELS)]

    def node_table(self):
        def frac(node, cells):
            return (2 * node * 2**32 + cells) // (2 * cells)

        xs = [frac(r, g) for g, n in zip(self.gx, self.nx) for r in range(n)]
        hs = [frac(c, g) for g, n, c in zip(self.gy, self.nx, self.ny) for r in range(n)]
        pad = [0] * (HALO - len(xs))
        ys = [frac(r, g) for g, n in zip(self.gy, self.ny) for r in range(n)]
        zs = [frac(r, g) for g in self.gz for r in range(g)]
        flat = np.array(xs + pad + hs + pad + ys + zs, np.int64) + 2**31
        flat = ((flat + 2**31) % 2**32 - 2**31).astype(np.int32)
        return np.repeat(flat[:, None], LANES, axis=1)

    def factor_table(self):
        k = [exponent(g) for g, n in zip(self.gx, self.nx) for _ in range(n)]
        h = [exponent(g) for g, n in zip(self.gy, self.nx) for _ in range(n)]
        pad = [0.0] * (HALO - len(k))
        return np.repeat(np.array(k + pad + h + pad, np.float32)[:, None], LANES, axis=1)

    def y_matrix(self, l):
        fine = self.rows[1]
        nx, ny, main = self.nx[l], self.ny[l], self.main[l]
        b = np.arange(fine)[:, None]
        y = np.arange(ny + 1)[None, :]
        hat = np.maximum(0.0, 1.0 - np.abs(y - b * self.gy[l] / FINE_Y))
        out = np.zeros((nx * fine, self.block[l]), np.float32)
        for x in range(nx):
            out[x * fine : (x + 1) * fine, x * ny : (x + 1) * ny] = hat[:, :ny]
            out[x * fine : (x + 1) * fine, main + self.xrow[l] + x] = hat[:, ny]
        return np.concatenate([out, out], axis=1)

    def x_matrix(self, l):
        a = np.arange(self.rows[0])[:, None]
        x = np.arange(self.nx[l])[None, :]
        return np.maximum(0.0, 1.0 - np.abs(x - a * self.gx[l] / FINE_X))


def exponent(cells):
    return -0.5 * np.log2(np.e) / spread_width**2 * (cells / 2.0**32) ** 2


def split(value):
    high = value.astype(jnp.bfloat16)
    low = (value - high.astype(jnp.float32)).astype(jnp.bfloat16)
    return high, low


def kernel(
    plan, cx, cy, cz, off, charge, count, amp, dens, nodes, factors, my0, my1, my2, my3,
    field, energy,
    buf, planes, wz, wy, wx, acc, other, pz, t2, dens_v, field_v, ez, ex,
    zs_sem, zr_sem, xs_sem, xr_sem, ps_sem, pr_sem, es_sem, er_sem, fs_sem, fr_sem, d_sem, o_sem,
):
    slabs, cols = plan.slabs, plan.cols
    half = slabs // 2
    me = lax.axis_index("slab")
    col = lax.axis_index("blk")
    core = lax.axis_index("sub")
    mats = (my0, my1, my2, my3)
    wide = 2 * BQ

    def at(ds, dc, dk):
        return {
            "slab": lax.rem(me + slabs + ds, slabs),
            "blk": lax.rem(col + cols + dc, cols),
            "sub": lax.rem(core + dk, 2),
        }

    order = [0]
    for d in range(1, half):
        order += [d, -d]
    order.append(half)
    others = [(dc, dk) for dc in range(cols) for dk in range(2)][1:]

    barrier = pltpu.get_barrier_semaphore()
    for ds in order[1:]:
        pl.semaphore_signal(barrier, inc=1, device_id=at(ds, 0, 0), device_id_type=MESH)
    for dc, dk in others:
        pl.semaphore_signal(barrier, inc=1, device_id=at(0, dc, dk), device_id_type=MESH)

    load = pltpu.make_async_copy(dens, dens_v, d_sem)
    load.start()

    lane = lax.broadcasted_iota(jnp.int32, (1, BQ), 1)
    live = jnp.where(lane < count[0], 1.0, 0.0).astype(jnp.float32)
    buf[0, 0, 0:1, 0:BQ] = charge[...] * live
    buf[0, 0, 1:2, 0:BQ] = cx[...].astype(jnp.float32) + off[0:1, :]
    buf[0, 0, 2:3, 0:BQ] = cy[...].astype(jnp.float32) + off[1:2, :]
    buf[0, 0, 3:4, 0:BQ] = cz[...].astype(jnp.float32) + off[2:3, :]
    acc[...] = jnp.zeros_like(acc)

    node = lax.broadcasted_iota(jnp.int32, (LANES, LANES), 0)
    fine = lax.broadcasted_iota(jnp.int32, (LANES, LANES), 1) + core * LANES
    for l in range(LEVELS):
        g = plan.gz[l]
        moved = node * FINE_Z - fine * g
        moved = jnp.where(moved < 0, moved + g * FINE_Z, moved)
        moved = jnp.where(moved * 2 >= g * FINE_Z, moved - g * FINE_Z, moved)
        hat = jnp.maximum(0.0, 1.0 - jnp.abs(moved.astype(jnp.float32)) * (1.0 / FINE_Z))
        hat = jnp.where(node < g, hat, 0.0).astype(jnp.bfloat16)
        pz[l, 0:LANES, :] = hat
        pz[l, LANES:, :] = hat

    pl.semaphore_wait(barrier, len(order) - 1 + len(others))

    def z_copy(k):
        row, part = k // 2, k % 2
        slot = buf.at[0, row, :, part * BQ : (part + 1) * BQ]
        return pltpu.make_async_remote_copy(
            src_ref=buf.at[0, 0, :, 0:BQ], dst_ref=slot, send_sem=zs_sem.at[k], recv_sem=zr_sem.at[k],
            device_id=at(-order[k], 0, 0), device_id_type=MESH,
        )

    for k in range(slabs - 1, 0, -1):
        z_copy(k).start()

    def z_wait(j, part):
        pltpu.make_async_remote_copy(
            src_ref=buf.at[0, 0, :, 0:BQ], dst_ref=buf.at[0, j, :, part * BQ : (part + 1) * BQ],
            send_sem=zs_sem.at[2 * j + part], recv_sem=zr_sem.at[2 * j + part],
            device_id=at(1, 0, 0), device_id_type=MESH,
        ).wait_recv()

    def x_copy(p, j):
        return pltpu.make_async_remote_copy(
            src_ref=buf.at[0, j], dst_ref=buf.at[p, j], send_sem=xs_sem.at[p, j], recv_sem=xr_sem.at[p, j],
            device_id=at(0, -p, 0), device_id_type=MESH,
        )

    scale = 2.0**32
    top = 2.0**31 - 128.0

    def fixed(row, cells):
        moved = jnp.minimum((row - 0.5 * cells) * (scale / cells), top)
        return moved.astype(jnp.int32)

    def gauss(first, rows, at_row, factor):
        table = nodes[first : first + rows, :]
        wrapped = (jnp.concatenate([table] * (wide // LANES), axis=1) - at_row).astype(jnp.float32)
        return jnp.exp2(wrapped * wrapped * factor)

    def spread(p, j):
        chunk = buf[p, j]
        ux = fixed(chunk[1:2, :], G0X) - me * (2**32 // slabs)
        uy = fixed(chunk[2:3, :], G0Y) - col * (2**32 // cols)
        uz = fixed(chunk[3:4, :], G0Z)
        fx = jnp.concatenate([factors[0:HALO, :]] * (wide // LANES), axis=1)
        fh = jnp.concatenate([factors[HALO : 2 * HALO, :]] * (wide // LANES), axis=1)
        weighted = chunk[0:1, :] * gauss(0, HALO, ux, fx)
        wx[...] = weighted
        edge = (weighted * gauss(HALO, HALO, uy, fh)).astype(jnp.bfloat16)
        for l in range(LEVELS):
            start, main = plan.start[l], plan.main[l]
            planes[start + main : start + main + HALO, :] = edge
            z0 = 2 * HALO + plan.yrow[-1] + plan.ny[-1] + plan.zrow[l]
            for r in range(0, plan.gz[l], 16):
                part = gauss(z0 + r, 16, uz, exponent(plan.gz[l])).astype(jnp.bfloat16)
                wz[plan.zrow[l] + r : plan.zrow[l] + r + 16, :] = part
            ny = plan.ny[l]
            along_y = gauss(2 * HALO + plan.yrow[l], ny, uy, exponent(plan.gy[l]))
            step = 1 if ny % 16 == 0 else 2
            for x in range(0, plan.nx[l], step):
                both = [wx[plan.xrow[l] + x + i : plan.xrow[l] + x + i + 1, :] * along_y for i in range(step)]
                value = both[0] if step == 1 else jnp.concatenate(both, axis=0)
                planes[start + x * ny : start + (x + step) * ny, :] = value.astype(jnp.bfloat16)
            rows = plan.block[l]
            acc[start : start + rows, 0 : plan.gz[l]] += lax.dot_general(
                planes[start : start + rows, :], wz[plan.zrow[l] : plan.zrow[l] + plan.gz[l], :],
                (((1,), (1,)), ((), ())), preferred_element_type=jnp.float32,
            )

    @pl.loop(0, half + 1)
    def _(j):
        @pl.when(j < half)
        def _():
            @pl.when(j > 0)
            def _():
                z_wait(j, 0)

            z_wait(j, 1)
            for p in range(1, cols):
                x_copy(p, j).start()

        @pl.loop(0, cols)
        def _(p):
            held = jnp.where(p == 0, j, j - 1)

            @pl.when((held >= 0) & (held < half))
            def _():
                @pl.when(p > 0)
                def _():
                    x_copy(p, held).wait_recv()

                spread(p, held)

    swap = pltpu.make_async_remote_copy(
        src_ref=acc, dst_ref=other, send_sem=ps_sem, recv_sem=pr_sem, device_id=at(0, 0, 1), device_id_type=MESH
    )
    swap.start()
    load.wait()
    swap.wait_recv()

    fine_y = plan.rows[1]
    for l in range(LEVELS):
        start, rows = plan.start[l], plan.block[l]
        cube = acc[start : start + rows, :] + other[start : start + rows, :]
        along_z = jnp.dot(jnp.concatenate(split(cube), axis=1), pz[l], preferred_element_type=jnp.float32)
        t2[plan.xrow[l] * fine_y : (plan.xrow[l] + plan.nx[l]) * fine_y, :] = amp[l] * jnp.dot(
            mats[l][...], jnp.concatenate(split(along_z), axis=0), preferred_element_type=jnp.float32
        )

    sums = jnp.zeros((fine_y, LANES), jnp.float32)
    for a in range(plan.rows[0]):
        value = None
        for l in range(LEVELS):
            hat = plan.x_matrix(l)[a]
            for x in range(plan.nx[l]):
                if hat[x] > 0.0:
                    at_x = (plan.xrow[l] + x) * fine_y
                    term = float(hat[x]) * t2[at_x : at_x + fine_y, :]
                    value = term if value is None else value + term
        field_v[a] = value
        sums = sums + value * dens_v[a]
    store = pltpu.make_async_copy(field_v, field, o_sem)
    store.start()

    ez[0] = jnp.sum(sums, axis=0, keepdims=True)

    def e_copy(k):
        return pltpu.make_async_remote_copy(
            src_ref=ez.at[0], dst_ref=ez.at[k], send_sem=es_sem.at[k], recv_sem=er_sem.at[k],
            device_id=at(-order[k], 0, 0), device_id_type=MESH,
        )

    for k in range(slabs - 1, 0, -1):
        e_copy(k).start()
    for k in range(1, slabs):
        e_copy(k).wait_recv()
    ex[0] = jnp.sum(ez[...], axis=0)

    def f_copy(k):
        dc, dk = others[k - 1]
        return pltpu.make_async_remote_copy(
            src_ref=ex.at[0], dst_ref=ex.at[k], send_sem=fs_sem.at[k], recv_sem=fr_sem.at[k],
            device_id=at(0, -dc, dk), device_id_type=MESH,
        )

    for k in range(len(others), 0, -1):
        f_copy(k).start()
    for k in range(1, len(others) + 1):
        f_copy(k).wait_recv()
    energy[0, 0] = jnp.sum(jnp.sum(ex[...], axis=0)) * (1.0 / (FINE_X * FINE_Y * FINE_Z))

    for k in range(1, slabs):
        z_copy(k).wait_send()
        e_copy(k).wait_send()

    @pl.loop(0, half)
    def _(j):
        for p in range(1, cols):
            x_copy(p, j).wait_send()

    for k in range(1, len(others) + 1):
        f_copy(k).wait_send()
    swap.wait_send()
    store.wait()


def on_device(cell_x, cell_y, cell_z, offsets, charge, block_count, level_amplitude, density):
    slabs, cols = lax.axis_size("slab"), lax.axis_size("blk")
    plan = Plan(slabs, cols, *density.shape)
    slots = cell_x.shape[0]
    mats = [jnp.asarray(plan.y_matrix(l), jnp.bfloat16) for l in range(LEVELS)]
    vmem = pl.BlockSpec(memory_space=pltpu.VMEM)
    smem = pl.BlockSpec(memory_space=pltpu.SMEM)
    anywhere = pl.BlockSpec(memory_space=pl.ANY)
    dma = pltpu.SemaphoreType.DMA
    field, energy = pl.pallas_call(
        functools.partial(kernel, plan),
        out_shape=(jax.ShapeDtypeStruct(density.shape, jnp.float32), jax.ShapeDtypeStruct((1, 1), jnp.float32)),
        in_specs=[vmem] * 5 + [smem] * 2 + [anywhere] + [vmem] * 6,
        out_specs=(anywhere, smem),
        scratch_shapes=[
            pltpu.VMEM((cols, slabs // 2, 4, 2 * BQ), jnp.float32),
            pltpu.VMEM((plan.total, 2 * BQ), jnp.bfloat16),
            pltpu.VMEM((sum(plan.gz), 2 * BQ), jnp.bfloat16),
            pltpu.VMEM((sum(plan.ny), 2 * BQ), jnp.float32),
            pltpu.VMEM((HALO, 2 * BQ), jnp.float32),
            pltpu.VMEM((plan.total, LANES), jnp.float32),
            pltpu.VMEM((plan.total, LANES), jnp.float32),
            pltpu.VMEM((LEVELS, 2 * LANES, LANES), jnp.bfloat16),
            pltpu.VMEM((sum(plan.nx) * density.shape[1], LANES), jnp.float32),
            pltpu.VMEM(density.shape, jnp.float32),
            pltpu.VMEM(density.shape, jnp.float32),
            pltpu.VMEM((slabs, 1, LANES), jnp.float32),
            pltpu.VMEM((2 * cols, 1, LANES), jnp.float32),
            dma((slabs,)), dma((slabs,)),
            dma((cols, slabs // 2)), dma((cols, slabs // 2)),
            dma, dma,
            dma((slabs,)), dma((slabs,)),
            dma((2 * cols,)), dma((2 * cols,)),
            dma, dma,
        ],
        compiler_params=pltpu.CompilerParams(collective_id=0, has_side_effects=True),
    )(
        cell_x.reshape(1, slots), cell_y.reshape(1, slots), cell_z.reshape(1, slots), offsets,
        charge.reshape(1, slots), block_count, level_amplitude, density,
        jnp.asarray(plan.node_table()), jnp.asarray(plan.factor_table()), *mats,
    )
    return field, energy.reshape(1)


def solution(mesh):
    split_all = ("grp", "slab", "blk", "sub")
    in_specs = (
        P(split_all), P(split_all), P(split_all), P(None, split_all), P(split_all), P(split_all), P(),
        P(("grp", "slab"), "blk", "sub"),
    )
    out_specs = (P(("grp", "slab"), "blk", "sub"), P("grp"))
    return jax.shard_map(on_device, mesh=mesh, in_specs=in_specs, out_specs=out_specs, check_vma=False)
```

time: 215 us -> 69.7 us (0.32)
  blocking collectives: 137 us -> 0 us
  Pallas kernels: 0 us -> 64.7 us
  matrix products: 28.8 us -> 0 us
  other arithmetic: 21.5 us -> 0 us
  between operations: 16.9 us -> 2.98 us
  local copies, waits for them, and re-layouts: 5.18 us -> 1.89 us
    all_gather x4 -> x0, blocking collectives: 91.9 us -> none  [the longest x3 49.4 us: over_pieces(): return lax.all_gather(value, axis).sum(0)]
    pallas_call x0 -> x1, Pallas kernels: none -> 64.7 us  [on_device(): pl.pallas_call(functools.partial(kernel, plan), out_shape=(jax.ShapeDtype...]
    psum x3 -> x0, blocking collectives: 44.9 us -> none  [by_axis(): return functools.reduce(lax.psum, axes, value)]
    dot_general x76 -> x0, matrix products: 28.8 us -> none  [the longest x64 14.4 us: spread_slab(): lax.dot_general(planes, along_z.astype(jnp.bfloat16), (((0,), (0,)), ((),...]
    mul x146 -> x0, other arithmetic: 7.69 us -> none  [the longest x64 5.47 us: spread_slab(): weighted[:, None] * along_x]
    convert_element_type x48 -> x0, other arithmetic: 5.89 us -> none  [spread_slab(): planes = ((weighted[:, None] * along_x)[:, :, None] * along_y[:, None, :]...]
    exp x48 -> x0, other arithmetic: 3.62 us -> none  [axis_weights(): return jnp.exp(-0.5 * (distance / spread_width) ** 2)]
    add x51 -> x0, other arithmetic: 2.42 us -> none  [the longest x1 0.69 us: on_device(): placed_x = cell_x.astype(jnp.float32) + offsets[0]]
  transfers between devices with their start and end apart: 5 -> 0, of which waited for: 1 -> 0; matrix products, arithmetic and copies ran while one was open for 4% -> 0% of each run, Pallas kernels for 0% -> 0%
where the time goes in v1:
time: 69.7 us; the launch traced here: 69.5 us
  Pallas kernels  64.7 us (93%)
  between operations  2.98 us (4%)
  local copies, waits for them, and re-layouts  1.89 us (3%)
    pallas_call x1, Pallas kernels, on_device(): pl.pallas_call(functools.partial(kernel, plan), out_shape=(jax.ShapeDtype...  64.7 us
    unnamed x1, local copies, waits for them, and re-layouts  1.89 us

profile of v1, /device:TPU:33, one launch (start us, length us, event | category | flops | bytes accessed | tf_op | source)
XLA Modules:
  0.0 69.5 jit_solution(17138841065695603547)
XLA Ops:
  1.3 64.7 %shard_map.149 = (f32[16,64,128]{2,1,0:T(8,128)}, f32[1,1]{1,0:T(1,128)}) custom-call(s32[1,256]{1,0:T(1,128)} %bitcast.5, s32[1,256]{1,0:T(1,128)} %bitcast.6, s32[1,256]{1,0:T(1,128)} %bitcast.7, f32[3,256]{1,0:T(4,128)} %off.1, f32[1,256]{1,0:T(1,128)} %bitcast.8, s32[1]{0:T(128)S(6)} %copy.18.count, f32[4]{0:T(128)} %amp.1, f32[16,64,128]{2,1,0:T(8,128)} %dens.1, ...), custom_call_target="tpu_custom_call" | custom-call | tf_op jit(solution)/shard_map/pallas_call | solution.py:323
  66.0 1.9 %copy.19 = f32[16,64,128]{2,1,0:T(8,128)} copy(f32[16,64,128]{2,1,0:T(8,128)} %get-tuple-element.8) | data formatting | bytes 1048576

commit v2 on v1

v2 whole, which is shorter than its diff:
```python
import functools

import jax
import jax.numpy as jnp
import numpy as np
from jax import lax
from jax.experimental import pallas as pl
from jax.experimental.pallas import tpu as pltpu
from jax.sharding import PartitionSpec as P

G0X = 64
G0Y = 128
G0Z = 128
FINE_X = 256
FINE_Y = 256
FINE_Z = 256
BQ = 256
LEVELS = 4
LANES = 128
SPAN = 256
ROWS = 8
HALO = 16
spread_width = 1.25
MESH = pl.DeviceIdType.MESH

ORDER = ((0, 2, 1, 3), (0, 1, 2), (0, 1), (0,))
SETS = (
    ((3, 0), ((3, 0, 1.0), (2, 0, 4.0), (1, 0, 9.0), (0, 0, 16.0))),
    ((2, 1), ((2, 1, 1.0), (0, 1, 4.0))),
    ((1, 1), ((1, 1, 1.0),)),
    ((1, 2), ((1, 2, 1.0),)),
    ((0, 1), ((0, 2, 1.0),)),
    ((0, 3), ((0, 3, 1.0),)),
)


def coarse_cells(base, level):
    return base * (4 - level) // 4


def exponent(cells):
    return -0.5 * np.log2(np.e) / spread_width**2 * (cells / 2.0**32) ** 2


class Plan:
    def __init__(self, slabs, cols, rows_x, rows_y, rows_z):
        self.slabs, self.cols = slabs, cols
        self.rows = (rows_x, rows_y, rows_z)
        self.gx = [coarse_cells(G0X, l) for l in range(LEVELS)]
        self.gy = [coarse_cells(G0Y, l) for l in range(LEVELS)]
        self.gz = [coarse_cells(G0Z, l) for l in range(LEVELS)]
        self.nx = [g // slabs + 1 for g in self.gx]
        self.ny = [g // cols for g in self.gy]
        self.main = [a * b for a, b in zip(self.nx, self.ny)]
        self.block = [m + HALO for m in self.main]
        self.start = [sum(self.block[:l]) for l in range(LEVELS)]
        self.total = sum(self.block)
        self.xrow = [sum(self.nx[:l]) for l in range(LEVELS)]
        self.yrow = [sum(self.ny[:l]) for l in range(LEVELS)]
        self.zrow = [sum(self.gz[:l]) for l in range(LEVELS)]
        self.yset, self.zset = self.ny[-1], self.gz[-1]
        self.ytable = 2 * HALO
        self.ztable = self.ytable + len(SETS) * self.yset

    def y_nodes(self, l):
        m = LEVELS - l
        return [m * k + s for s in ORDER[l] for k in range(self.yset)]

    def node_table(self):
        def frac(node, cells):
            return (2 * node * 2**32 + cells) // (2 * cells)

        flat = [frac(r, g) for g, n in zip(self.gx, self.nx) for r in range(n)]
        flat += [0] * (HALO - len(flat))
        flat += [frac(c, g) for g, n, c in zip(self.gy, self.nx, self.ny) for _ in range(n)]
        flat += [0] * (2 * HALO - len(flat))
        for cells, count in ((self.gy, self.yset), (self.gz, self.zset)):
            for (l, s), _ in SETS:
                flat += [frac((LEVELS - l) * k + s, cells[l]) for k in range(count)]
        flat = np.array(flat, np.int64) + 2**31
        flat = ((flat + 2**31) % 2**32 - 2**31).astype(np.int32)
        return np.repeat(flat[:, None], LANES, axis=1)

    def factor_table(self):
        k = [exponent(g) for g, n in zip(self.gx, self.nx) for _ in range(n)]
        h = [exponent(g) for g, n in zip(self.gy, self.nx) for _ in range(n)]
        pad = [0.0] * (HALO - len(k))
        return np.repeat(np.array(k + pad + h + pad, np.float32)[:, None], LANES, axis=1)

    def y_matrix(self, l):
        fine = self.rows[1]
        nx, ny, main = self.nx[l], self.ny[l], self.main[l]
        b = np.arange(fine)[:, None]
        y = np.array(self.y_nodes(l) + [ny])[None, :]
        hat = np.maximum(0.0, 1.0 - np.abs(y - b * self.gy[l] / FINE_Y))
        out = np.zeros((nx * fine, self.block[l]), np.float32)
        for x in range(nx):
            out[x * fine : (x + 1) * fine, x * ny : (x + 1) * ny] = hat[:, :ny]
            out[x * fine : (x + 1) * fine, main + self.xrow[l] + x] = hat[:, ny]
        return out

    def x_matrix(self, l):
        a = np.arange(self.rows[0])[:, None]
        x = np.arange(self.nx[l])[None, :]
        return np.maximum(0.0, 1.0 - np.abs(x - a * self.gx[l] / FINE_X))

    def constants(self):
        twice = lambda m: jnp.asarray(np.concatenate([m, m], axis=1), jnp.bfloat16)
        down = [twice(self.y_matrix(l)) for l in range(LEVELS)]
        up = [twice(self.y_matrix(l).T) for l in range(LEVELS)]
        return [jnp.asarray(self.node_table()), jnp.asarray(self.factor_table())] + down + up


def split(value):
    high = value.astype(jnp.bfloat16)
    low = (value - high.astype(jnp.float32)).astype(jnp.bfloat16)
    return high, low


def kernel(plan, n_in, *refs):
    hbm, refs = refs[:n_in], refs[n_in:]
    field, energy, refs = refs[0], refs[1], refs[2:]
    held_in, refs = refs[:n_in], refs[n_in:]
    (
        buf, planes, wz, acc, other, dual, dual_other, pz, t2, field_v, ez, ex,
        in_sem, zs_sem, zr_sem, xs_sem, xr_sem, ps_sem, pr_sem, es_sem, er_sem, fs_sem, fr_sem, o_sem,
    ) = refs
    cx, cy, cz, off, charge, count, amp, dens_v, nodes, factors = held_in[:10]
    down, up = held_in[10 : 10 + LEVELS], held_in[10 + LEVELS :]
    slabs, cols = plan.slabs, plan.cols
    half = slabs // 2
    reach = half // 2
    me = lax.axis_index("slab")
    col = lax.axis_index("blk")
    core = lax.axis_index("sub")
    wide = 2 * BQ
    fine_y = plan.rows[1]

    def at(ds, dc, dk):
        return {
            "slab": lax.rem(me + slabs + ds, slabs),
            "blk": lax.rem(col + cols + dc, cols),
            "sub": lax.rem(core + dk, 2),
        }

    order = [0]
    for d in range(1, half):
        order += [d, -d]
    order.append(half)
    others = [(dc, dk) for dc in range(cols) for dk in range(2)][1:]

    barrier = pltpu.get_barrier_semaphore()
    near = order[1 : 2 * reach] + [reach, -reach]
    near = [d for i, d in enumerate(near) if d not in near[:i]]
    for ds in near:
        pl.semaphore_signal(barrier, inc=1, device_id=at(ds, 0, 0), device_id_type=MESH)
    for dc, dk in others:
        pl.semaphore_signal(barrier, inc=1, device_id=at(0, dc, dk), device_id_type=MESH)

    loads = [pltpu.make_async_copy(hbm[i], held_in[i], in_sem.at[i]) for i in range(n_in)]
    for load in loads:
        load.start()
    for i in range(6):
        loads[i].wait()

    lane = lax.broadcasted_iota(jnp.int32, (1, BQ), 1)
    live = jnp.where(lane < count[0], 1.0, 0.0).astype(jnp.float32)
    buf[0, 0, 0:1, 0:BQ] = charge[...] * live
    buf[0, 0, 1:2, 0:BQ] = cx[...].astype(jnp.float32) + off[0:1, :]
    buf[0, 0, 2:3, 0:BQ] = cy[...].astype(jnp.float32) + off[1:2, :]
    buf[0, 0, 3:4, 0:BQ] = cz[...].astype(jnp.float32) + off[2:3, :]

    pl.semaphore_wait(barrier, len(near) + len(others))

    def slot(j, part):
        return buf.at[0, j, :, pl.ds(part * BQ, BQ)]

    def z_copy(src, j, part, ds):
        return pltpu.make_async_remote_copy(
            src_ref=src, dst_ref=slot(j, part), send_sem=zs_sem.at[j, part], recv_sem=zr_sem.at[j, part],
            device_id=at(ds, 0, 0), device_id_type=MESH,
        )

    for k in range(2 * reach, 0, -1):
        z_copy(slot(0, 0), k // 2, k % 2, -order[k]).start()

    def x_copy(p, j):
        return pltpu.make_async_remote_copy(
            src_ref=buf.at[0, j], dst_ref=buf.at[p, j], send_sem=xs_sem.at[p, j], recv_sem=xr_sem.at[p, j],
            device_id=at(0, -p, 0), device_id_type=MESH,
        )

    acc[...] = jnp.zeros_like(acc)
    planes[1] = jnp.zeros(planes.shape[1:], planes.dtype)
    wz[1] = jnp.zeros(wz.shape[1:], wz.dtype)

    row = lax.broadcasted_iota(jnp.int32, (LANES, LANES), 0)
    fine = lax.broadcasted_iota(jnp.int32, (LANES, LANES), 1) + core * LANES
    for l in range(LEVELS):
        g = plan.gz[l]
        place = row // plan.zset
        part = (place % 2) * 2 + place // 2 if l == 0 else place
        node = (row % plan.zset) * (LEVELS - l) + part
        moved = node * FINE_Z - fine * g
        moved = jnp.where(moved < 0, moved + g * FINE_Z, moved)
        moved = jnp.where(moved * 2 >= g * FINE_Z, moved - g * FINE_Z, moved)
        hat = jnp.maximum(0.0, 1.0 - jnp.abs(moved.astype(jnp.float32)) * (1.0 / FINE_Z))
        hat = jnp.where(row < g, hat, 0.0).astype(jnp.bfloat16)
        pz[l, 0:LANES, :] = hat
        pz[l, LANES:, :] = hat

    for i in range(6, n_in):
        loads[i].wait()
    for l in range(LEVELS):
        hats = plan.x_matrix(l)
        for x in range(plan.nx[l]):
            value = None
            for a in range(plan.rows[0]):
                if hats[a, x] > 0.0:
                    term = float(hats[a, x]) * dens_v[a]
                    value = term if value is None else value + term
            at_x = (plan.xrow[l] + x) * fine_y
            t2[at_x : at_x + fine_y, :] = value * amp[l]
        start, rows = plan.start[l], plan.block[l]
        along = t2[plan.xrow[l] * fine_y : (plan.xrow[l] + plan.nx[l]) * fine_y, :]
        on_y = jnp.dot(up[l][...], jnp.concatenate(split(along), axis=0), preferred_element_type=jnp.float32)
        both = lax.dot_general(
            jnp.concatenate(split(on_y), axis=0), pz[l, 0:LANES, :], (((1,), (1,)), ((), ())),
            preferred_element_type=jnp.float32,
        )
        dual[start : start + rows, :] = both[:rows] + both[rows:]

    def swap(k, src, dst):
        return pltpu.make_async_remote_copy(
            src_ref=src, dst_ref=dst, send_sem=ps_sem.at[k], recv_sem=pr_sem.at[k],
            device_id=at(0, 0, 1), device_id_type=MESH,
        )

    swap(0, dual, dual_other).start()

    scale = 2.0**32
    top = 2.0**31 - 128.0

    def fixed(line, cells):
        moved = jnp.minimum((line - 0.5 * cells) * (scale / cells), top)
        return moved.astype(jnp.int32)

    def broad(table):
        return jnp.concatenate([table] * (SPAN // LANES), axis=1)

    def weigh(p, j, s):
        for c in range(0, wide, SPAN):
            lanes = slice(c, c + SPAN)
            chunk = buf[p, j, :, lanes]
            ux = fixed(chunk[1:2, :], G0X) - me * (2**32 // slabs)
            uy = fixed(chunk[2:3, :], G0Y) - col * (2**32 // cols)
            uz = fixed(chunk[3:4, :], G0Z)

            def squared(first, rows, at_line, factor):
                wrapped = (broad(nodes[first : first + rows, :]) - at_line).astype(jnp.float32)
                return wrapped * wrapped * factor

            for i, ((l0, _), uses) in enumerate(SETS):
                for r in range(0, plan.zset, ROWS):
                    power = squared(plan.ztable + i * plan.zset + r, ROWS, uz, exponent(plan.gz[l0]))
                    for l, place, times in uses:
                        value = jnp.exp2(power if times == 1.0 else power * times).astype(jnp.bfloat16)
                        to = plan.zrow[l] + place * plan.zset + r
                        wz[s, to : to + ROWS, lanes] = value
            along_y = [[None] * len(ORDER[l]) for l in range(LEVELS)]
            for i, ((l0, _), uses) in enumerate(SETS):
                power = squared(plan.ytable + i * plan.yset, plan.yset, uy, exponent(plan.gy[l0]))
                for l, place, times in uses:
                    along_y[l][place] = jnp.exp2(power if times == 1.0 else power * times)
            weighted = chunk[0:1, :] * jnp.exp2(squared(0, HALO, ux, broad(factors[0:HALO, :])))
            last = jnp.exp2(squared(HALO, HALO, uy, broad(factors[HALO : 2 * HALO, :])))
            edge = (weighted * last).astype(jnp.bfloat16)
            for l in range(LEVELS):
                start, main, ny = plan.start[l], plan.main[l], plan.ny[l]
                planes[s, start + main : start + main + HALO, lanes] = edge
                tiles = [
                    weighted[plan.xrow[l] + x : plan.xrow[l] + x + 1, :] * on_y
                    for x in range(plan.nx[l]) for on_y in along_y[l]
                ]
                for t, tile in enumerate(tiles):
                    to = start + t * plan.yset
                    planes[s, to : to + plan.yset, lanes] = tile.astype(jnp.bfloat16)

    def gather_in(s):
        for l in range(LEVELS):
            start, rows = plan.start[l], plan.block[l]
            acc[start : start + rows, 0 : plan.gz[l]] += lax.dot_general(
                planes[s, start : start + rows, :], wz[s, plan.zrow[l] : plan.zrow[l] + plan.gz[l], :],
                (((1,), (1,)), ((), ())), preferred_element_type=jnp.float32,
            )

    def arrive(j):
        pair = half // 2

        @pl.when(j > 0)
        def _():
            z_copy(slot(0, 0), j, 0, 1).wait_recv()

        z_copy(slot(0, 0), j, 1, 1).wait_recv()

        @pl.when((j > 0) & (j < pair))
        def _():
            z_copy(slot(j, 0), j + pair, 0, reach).start()

        @pl.when(j < pair)
        def _():
            z_copy(slot(j, 1), j + pair, 1, -reach).start()

        for p in range(1, cols):
            x_copy(p, j).start()

    steps = half // 2

    @pl.loop(0, steps + 1)
    def _(m):
        @pl.when(m < steps)
        def _():
            arrive(2 * m)
            arrive(2 * m + 1)

        @pl.loop(0, cols)
        def _(p):
            held = jnp.where(p == 0, m, m - 1)

            @pl.when((held >= 0) & (held < steps))
            def _():
                @pl.when(p > 0)
                def _():
                    x_copy(p, 2 * held).wait_recv()
                    x_copy(p, 2 * held + 1).wait_recv()

                gather_in(1)
                weigh(p, 2 * held, 0)
                gather_in(0)
                weigh(p, 2 * held + 1, 1)

    gather_in(1)
    swap(1, acc, other).start()
    swap(0, dual, dual_other).wait_recv()
    ez[0] = jnp.sum(acc[...] * (dual[...] + dual_other[...]), axis=0, keepdims=True)

    def e_copy(k):
        return pltpu.make_async_remote_copy(
            src_ref=ez.at[0], dst_ref=ez.at[k], send_sem=es_sem.at[k], recv_sem=er_sem.at[k],
            device_id=at(-order[k], 0, 0), device_id_type=MESH,
        )

    for k in range(slabs - 1, 0, -1):
        e_copy(k).start()
    swap(1, acc, other).wait_recv()

    for l in range(LEVELS):
        start, rows = plan.start[l], plan.block[l]
        cube = acc[start : start + rows, :] + other[start : start + rows, :]
        along_z = jnp.dot(jnp.concatenate(split(cube), axis=1), pz[l], preferred_element_type=jnp.float32)
        t2[plan.xrow[l] * fine_y : (plan.xrow[l] + plan.nx[l]) * fine_y, :] = amp[l] * jnp.dot(
            down[l][...], jnp.concatenate(split(along_z), axis=0), preferred_element_type=jnp.float32
        )
    for a in range(plan.rows[0]):
        value = None
        for l in range(LEVELS):
            hat = plan.x_matrix(l)[a]
            for x in range(plan.nx[l]):
                if hat[x] > 0.0:
                    at_x = (plan.xrow[l] + x) * fine_y
                    term = float(hat[x]) * t2[at_x : at_x + fine_y, :]
                    value = term if value is None else value + term
        field_v[a] = value
    store = pltpu.make_async_copy(field_v, field, o_sem)
    store.start()

    for k in range(1, slabs):
        e_copy(k).wait_recv()
    ex[0] = jnp.sum(ez[...], axis=0)

    def f_copy(k):
        dc, dk = others[k - 1]
        return pltpu.make_async_remote_copy(
            src_ref=ex.at[0], dst_ref=ex.at[k], send_sem=fs_sem.at[k], recv_sem=fr_sem.at[k],
            device_id=at(0, -dc, dk), device_id_type=MESH,
        )

    for k in range(len(others), 0, -1):
        f_copy(k).start()

    for k in range(1, slabs):
        z_copy(slot(0, 0), k // 2, k % 2, 1).wait_send()
        e_copy(k).wait_send()

    @pl.loop(0, half)
    def _(j):
        for p in range(1, cols):
            x_copy(p, j).wait_send()

    swap(0, dual, dual_other).wait_send()
    swap(1, acc, other).wait_send()
    store.wait()
    for k in range(1, len(others) + 1):
        f_copy(k).wait_recv()
    energy[0, 0] = jnp.sum(jnp.sum(ex[...], axis=0)) * (1.0 / (FINE_X * FINE_Y * FINE_Z))
    for k in range(1, len(others) + 1):
        f_copy(k).wait_send()


def on_device(cell_x, cell_y, cell_z, offsets, charge, block_count, level_amplitude, density):
    slabs, cols = lax.axis_size("slab"), lax.axis_size("blk")
    plan = Plan(slabs, cols, *density.shape)
    slots = cell_x.shape[0]
    operands = [
        cell_x.reshape(1, slots), cell_y.reshape(1, slots), cell_z.reshape(1, slots), offsets,
        charge.reshape(1, slots), block_count, level_amplitude, density, *plan.constants(),
    ]
    n_in = len(operands)
    spaces = [pltpu.VMEM] * 5 + [pltpu.SMEM] * 2 + [pltpu.VMEM] * (n_in - 7)
    smem = pl.BlockSpec(memory_space=pltpu.SMEM)
    anywhere = pl.BlockSpec(memory_space=pl.ANY)
    dma = pltpu.SemaphoreType.DMA
    field, energy = pl.pallas_call(
        functools.partial(kernel, plan, n_in),
        out_shape=(jax.ShapeDtypeStruct(density.shape, jnp.float32), jax.ShapeDtypeStruct((1, 1), jnp.float32)),
        in_specs=[anywhere] * n_in,
        out_specs=(anywhere, smem),
        scratch_shapes=[space(o.shape, o.dtype) for space, o in zip(spaces, operands)]
        + [
            pltpu.VMEM((cols, slabs // 2, 4, 2 * BQ), jnp.float32),
            pltpu.VMEM((2, plan.total, 2 * BQ), jnp.bfloat16),
            pltpu.VMEM((2, sum(plan.gz), 2 * BQ), jnp.bfloat16),
            pltpu.VMEM((plan.total, LANES), jnp.float32),
            pltpu.VMEM((plan.total, LANES), jnp.float32),
            pltpu.VMEM((plan.total, LANES), jnp.float32),
            pltpu.VMEM((plan.total, LANES), jnp.float32),
            pltpu.VMEM((LEVELS, 2 * LANES, LANES), jnp.bfloat16),
            pltpu.VMEM((sum(plan.nx) * density.shape[1], LANES), jnp.float32),
            pltpu.VMEM(density.shape, jnp.float32),
            pltpu.VMEM((slabs, 1, LANES), jnp.float32),
            pltpu.VMEM((2 * cols, 1, LANES), jnp.float32),
            dma((n_in,)),
            dma((slabs // 2, 2)), dma((slabs // 2, 2)),
            dma((cols, slabs // 2)), dma((cols, slabs // 2)),
            dma((2,)), dma((2,)),
            dma((slabs,)), dma((slabs,)),
            dma((2 * cols,)), dma((2 * cols,)),
            dma,
        ],
        compiler_params=pltpu.CompilerParams(collective_id=0, has_side_effects=True),
    )(*operands)
    return field, energy.reshape(1)


def solution(mesh):
    split_all = ("grp", "slab", "blk", "sub")
    in_specs = (
        P(split_all), P(split_all), P(split_all), P(None, split_all), P(split_all), P(split_all), P(),
        P(("grp", "slab"), "blk", "sub"),
    )
    out_specs = (P(("grp", "slab"), "blk", "sub"), P("grp"))
    return jax.shard_map(on_device, mesh=mesh, in_specs=in_specs, out_specs=out_specs, check_vma=False)
```

time: 69.7 us -> 59.4 us (0.85)
  Pallas kernels: 64.7 us -> 54.4 us
    pallas_call x1, Pallas kernels: 64.7 us -> 54.4 us  [on_device(): pl.pallas_call(functools.partial(kernel, plan, n_in), out_shape=(jax.Shap...]
where the time goes in v2:
time: 59.4 us; the launch traced here: 59.2 us
  Pallas kernels  54.4 us (92%)
  between operations  2.98 us (5%)
  local copies, waits for them, and re-layouts  1.89 us (3%)
    pallas_call x1, Pallas kernels, on_device(): pl.pallas_call(functools.partial(kernel, plan, n_in), out_shape=(jax.Shap...  54.4 us
    unnamed x1, local copies, waits for them, and re-layouts  1.89 us

profile of v2, /device:TPU:33, one launch (start us, length us, event | category | flops | bytes accessed | tf_op | source)
XLA Modules:
  0.0 59.2 jit_solution(9115452856933072960)
XLA Ops:
  1.3 54.4 %shard_map.185 = (f32[16,64,128]{2,1,0:T(8,128)}, f32[1,1]{1,0:T(1,128)}) custom-call(s32[1,256]{1,0:T(1,128)} %bitcast.5, s32[1,256]{1,0:T(1,128)} %bitcast.6, s32[1,256]{1,0:T(1,128)} %bitcast.7, f32[3,256]{1,0:T(4,128)} %refs_3_.1, f32[1,256]{1,0:T(1,128)} %bitcast.8, s32[1]{0:T(128)S(6)} %copy.22.refs_5_, f32[4]{0:T(128)} %refs_6_.1, ...), custom_call_target="tpu_custom_call" | custom-call | tf_op jit(solution)/shard_map/pallas_call | solution.py:423
  55.7 1.9 %copy.23 = f32[16,64,128]{2,1,0:T(8,128)} copy(f32[16,64,128]{2,1,0:T(8,128)} %get-tuple-element.8) | data formatting | bytes 1048576

commit v3 on v2

--- a/solution.py
+++ b/solution.py
@@ -122,7 +122,7 @@
     field, energy, refs = refs[0], refs[1], refs[2:]
     held_in, refs = refs[:n_in], refs[n_in:]
     (
-        buf, planes, wz, acc, other, dual, dual_other, pz, t2, field_v, ez, ex,
+        buf, planes, wz, wx, acc, other, dual, dual_other, pz, t2, field_v, ez, ex,
         in_sem, zs_sem, zr_sem, xs_sem, xr_sem, ps_sem, pr_sem, es_sem, er_sem, fs_sem, fr_sem, o_sem,
     ) = refs
     cx, cy, cz, off, charge, count, amp, dens_v, nodes, factors = held_in[:10]
@@ -164,7 +164,7 @@
         loads[i].wait()
 
     lane = lax.broadcasted_iota(jnp.int32, (1, BQ), 1)
-    live = jnp.where(lane < count[0], 1.0, 0.0).astype(jnp.float32)
+    live = jnp.where(lane < count[...], 1.0, 0.0).astype(jnp.float32)
     buf[0, 0, 0:1, 0:BQ] = charge[...] * live
     buf[0, 0, 1:2, 0:BQ] = cx[...].astype(jnp.float32) + off[0:1, :]
     buf[0, 0, 2:3, 0:BQ] = cy[...].astype(jnp.float32) + off[1:2, :]
@@ -274,12 +274,13 @@
                     along_y[l][place] = jnp.exp2(power if times == 1.0 else power * times)
             weighted = chunk[0:1, :] * jnp.exp2(squared(0, HALO, ux, broad(factors[0:HALO, :])))
             last = jnp.exp2(squared(HALO, HALO, uy, broad(factors[HALO : 2 * HALO, :])))
+            wx[s, :, lanes] = weighted
             edge = (weighted * last).astype(jnp.bfloat16)
             for l in range(LEVELS):
                 start, main, ny = plan.start[l], plan.main[l], plan.ny[l]
                 planes[s, start + main : start + main + HALO, lanes] = edge
                 tiles = [
-                    weighted[plan.xrow[l] + x : plan.xrow[l] + x + 1, :] * on_y
+                    wx[s, plan.xrow[l] + x : plan.xrow[l] + x + 1, lanes] * on_y
                     for x in range(plan.nx[l]) for on_y in along_y[l]
                 ]
                 for t, tile in enumerate(tiles):
@@ -315,29 +316,34 @@
             x_copy(p, j).start()
 
     steps = half // 2
-
-    @pl.loop(0, steps + 1)
-    def _(m):
-        @pl.when(m < steps)
+    far = steps // 2
+    turn = far + cols - 1
+    rest = turn + steps - far
+
+    @pl.loop(0, steps * cols)
+    def _(t):
+        early, late = t < far, t >= rest
+        own = early | ((t >= turn) & (t < rest))
+        p = jnp.where(own, 0, jnp.where(late, lax.rem(t + (cols - 1) * rest - rest, cols - 1) + 1, t - far + 1))
+        m = jnp.where(early, t, jnp.where(late, lax.div(t + (cols - 1) - rest, cols - 1), jnp.where(own, t - turn + far, 0)))
+
+        @pl.when((t == 0) | (t == turn))
         def _():
-            arrive(2 * m)
-            arrive(2 * m + 1)
-
-        @pl.loop(0, cols)
-        def _(p):
-            held = jnp.where(p == 0, m, m - 1)
-
-            @pl.when((held >= 0) & (held < steps))
-            def _():
-                @pl.when(p > 0)
-                def _():
-                    x_copy(p, 2 * held).wait_recv()
-                    x_copy(p, 2 * held + 1).wait_recv()
-
-                gather_in(1)
-                weigh(p, 2 * held, 0)
-                gather_in(0)
-                weigh(p, 2 * held + 1, 1)
+            first = jnp.where(t == 0, 0, 2 * far)
+
+            @pl.loop(0, 2 * far)
+            def _(j):
+                arrive(first + j)
+
+        @pl.when(p > 0)
+        def _():
+            x_copy(p, 2 * m).wait_recv()
+            x_copy(p, 2 * m + 1).wait_recv()
+
+        gather_in(1)
+        weigh(p, 2 * m, 0)
+        gather_in(0)
+        weigh(p, 2 * m + 1, 1)
 
     gather_in(1)
     swap(1, acc, other).start()
@@ -413,10 +419,10 @@
     slots = cell_x.shape[0]
     operands = [
         cell_x.reshape(1, slots), cell_y.reshape(1, slots), cell_z.reshape(1, slots), offsets,
-        charge.reshape(1, slots), block_count, level_amplitude, density, *plan.constants(),
+        charge.reshape(1, slots), block_count.reshape(1, 1), level_amplitude, density, *plan.constants(),
     ]
     n_in = len(operands)
-    spaces = [pltpu.VMEM] * 5 + [pltpu.SMEM] * 2 + [pltpu.VMEM] * (n_in - 7)
+    spaces = [pltpu.VMEM] * 6 + [pltpu.SMEM] + [pltpu.VMEM] * (n_in - 7)
     smem = pl.BlockSpec(memory_space=pltpu.SMEM)
     anywhere = pl.BlockSpec(memory_space=pl.ANY)
     dma = pltpu.SemaphoreType.DMA
@@ -430,6 +436,7 @@
             pltpu.VMEM((cols, slabs // 2, 4, 2 * BQ), jnp.float32),
             pltpu.VMEM((2, plan.total, 2 * BQ), jnp.bfloat16),
             pltpu.VMEM((2, sum(plan.gz), 2 * BQ), jnp.bfloat16),
+            pltpu.VMEM((2, HALO, 2 * BQ), jnp.float32),
             pltpu.VMEM((plan.total, LANES), jnp.float32),
             pltpu.VMEM((plan.total, LANES), jnp.float32),
             pltpu.VMEM((plan.total, LANES), jnp.float32),

time: 59.4 us -> 58.8 us (0.990)
  Pallas kernels: 54.4 us -> 53.8 us
    pallas_call x1, Pallas kernels: 54.4 us -> 53.8 us  [on_device(): pl.pallas_call(functools.partial(kernel, plan, n_in), out_shape=(jax.Shap...]
where the time goes in v3:
time: 58.8 us; the launch traced here: 58.6 us
  Pallas kernels  53.8 us (91%)
  between operations  2.98 us (5%)
  local copies, waits for them, and re-layouts  1.89 us (3%)
    pallas_call x1, Pallas kernels, on_device(): pl.pallas_call(functools.partial(kernel, plan, n_in), out_shape=(jax.Shap...  53.8 us
    unnamed x1, local copies, waits for them, and re-layouts  1.89 us

profile of v3, /device:TPU:33, one launch (start us, length us, event | category | flops | bytes accessed | tf_op | source)
XLA Modules:
  0.0 58.6 jit_solution(10394346076922389681)
XLA Ops:
  1.3 53.8 %shard_map.185 = (f32[16,64,128]{2,1,0:T(8,128)}, f32[1,1]{1,0:T(1,128)}) custom-call(s32[1,256]{1,0:T(1,128)} %bitcast.7, s32[1,256]{1,0:T(1,128)} %bitcast.8, s32[1,256]{1,0:T(1,128)} %bitcast.9, f32[3,256]{1,0:T(4,128)} %refs_3_.1, f32[1,256]{1,0:T(1,128)} %bitcast.10, s32[1,1]{1,0:T(1,128)} %bitcast.6.refs_5_, f32[4]{0:T(128)} %refs_6_.1, ...), custom_call_target="tpu_custom_call" | custom-call | tf_op jit(solution)/shard_map/pallas_call | solution.py:429
  55.0 1.9 %copy.23 = f32[16,64,128]{2,1,0:T(8,128)} copy(f32[16,64,128]{2,1,0:T(8,128)} %get-tuple-element.8) | data formatting | bytes 1048576

commit v4 on v3

--- a/solution.py
+++ b/solution.py
@@ -248,8 +248,8 @@
     def broad(table):
         return jnp.concatenate([table] * (SPAN // LANES), axis=1)
 
-    def weigh(p, j, s):
-        for c in range(0, wide, SPAN):
+    def weigh(p, j, s, beside):
+        for turn_of, c in enumerate(range(0, wide, SPAN)):
             lanes = slice(c, c + SPAN)
             chunk = buf[p, j, :, lanes]
             ux = fixed(chunk[1:2, :], G0X) - me * (2**32 // slabs)
@@ -267,11 +267,13 @@
                         value = jnp.exp2(power if times == 1.0 else power * times).astype(jnp.bfloat16)
                         to = plan.zrow[l] + place * plan.zset + r
                         wz[s, to : to + ROWS, lanes] = value
+            beside(2 * turn_of)
             along_y = [[None] * len(ORDER[l]) for l in range(LEVELS)]
             for i, ((l0, _), uses) in enumerate(SETS):
                 power = squared(plan.ytable + i * plan.yset, plan.yset, uy, exponent(plan.gy[l0]))
                 for l, place, times in uses:
                     along_y[l][place] = jnp.exp2(power if times == 1.0 else power * times)
+            beside(2 * turn_of + 1)
             weighted = chunk[0:1, :] * jnp.exp2(squared(0, HALO, ux, broad(factors[0:HALO, :])))
             last = jnp.exp2(squared(HALO, HALO, uy, broad(factors[HALO : 2 * HALO, :])))
             wx[s, :, lanes] = weighted
@@ -287,8 +289,8 @@
                     to = start + t * plan.yset
                     planes[s, to : to + plan.yset, lanes] = tile.astype(jnp.bfloat16)
 
-    def gather_in(s):
-        for l in range(LEVELS):
+    def gather_in(s, *levels):
+        for l in levels or range(LEVELS):
             start, rows = plan.start[l], plan.block[l]
             acc[start : start + rows, 0 : plan.gz[l]] += lax.dot_general(
                 planes[s, start : start + rows, :], wz[s, plan.zrow[l] : plan.zrow[l] + plan.gz[l], :],
@@ -320,30 +322,30 @@
     turn = far + cols - 1
     rest = turn + steps - far
 
-    @pl.loop(0, steps * cols)
-    def _(t):
+    @pl.loop(0, 2 * steps * cols)
+    def _(group):
+        t, half_of = lax.div(group, 2), lax.rem(group, 2)
         early, late = t < far, t >= rest
         own = early | ((t >= turn) & (t < rest))
         p = jnp.where(own, 0, jnp.where(late, lax.rem(t + (cols - 1) * rest - rest, cols - 1) + 1, t - far + 1))
         m = jnp.where(early, t, jnp.where(late, lax.div(t + (cols - 1) - rest, cols - 1), jnp.where(own, t - turn + far, 0)))
-
-        @pl.when((t == 0) | (t == turn))
+        j = 2 * m + half_of
+
+        @pl.when(early | (group == 2 * turn))
         def _():
-            first = jnp.where(t == 0, 0, 2 * far)
-
-            @pl.loop(0, 2 * far)
-            def _(j):
-                arrive(first + j)
+            @pl.loop(0, jnp.where(early, 1, 2 * (steps - far)))
+            def _(k):
+                arrive(j + k)
 
         @pl.when(p > 0)
         def _():
-            x_copy(p, 2 * m).wait_recv()
-            x_copy(p, 2 * m + 1).wait_recv()
-
-        gather_in(1)
-        weigh(p, 2 * m, 0)
-        gather_in(0)
-        weigh(p, 2 * m + 1, 1)
+            x_copy(p, j).wait_recv()
+
+        for s in range(2):
+
+            @pl.when(half_of == s)
+            def _():
+                weigh(p, j, s, lambda l: gather_in(1 - s, l))
 
     gather_in(1)
     swap(1, acc, other).start()

time: 58.8 us -> 59.8 us (1.017)
  Pallas kernels: 53.8 us -> 54.8 us
    pallas_call x1, Pallas kernels: 53.8 us -> 54.8 us  [on_device(): pl.pallas_call(functools.partial(kernel, plan, n_in), out_shape=(jax.Shap...]
where the time goes in v4:
time: 59.8 us; the launch traced here: 59.6 us
  Pallas kernels  54.8 us (92%)
  between operations  2.98 us (5%)
  local copies, waits for them, and re-layouts  1.89 us (3%)
    pallas_call x1, Pallas kernels, on_device(): pl.pallas_call(functools.partial(kernel, plan, n_in), out_shape=(jax.Shap...  54.8 us
    unnamed x1, local copies, waits for them, and re-layouts  1.89 us

profile of v4, /device:TPU:33, one launch (start us, length us, event | category | flops | bytes accessed | tf_op | source)
XLA Modules:
  0.0 59.6 jit_solution(3389091871306433411)
XLA Ops:
  1.3 54.8 %shard_map.185 = (f32[16,64,128]{2,1,0:T(8,128)}, f32[1,1]{1,0:T(1,128)}) custom-call(s32[1,256]{1,0:T(1,128)} %bitcast.7, s32[1,256]{1,0:T(1,128)} %bitcast.8, s32[1,256]{1,0:T(1,128)} %bitcast.9, f32[3,256]{1,0:T(4,128)} %refs_3_.1, f32[1,256]{1,0:T(1,128)} %bitcast.10, s32[1,1]{1,0:T(1,128)} %bitcast.6.refs_5_, f32[4]{0:T(128)} %refs_6_.1, ...), custom_call_target="tpu_custom_call" | custom-call | tf_op jit(solution)/shard_map/pallas_call | solution.py:431
  56.1 1.9 %copy.23 = f32[16,64,128]{2,1,0:T(8,128)} copy(f32[16,64,128]{2,1,0:T(8,128)} %get-tuple-element.8) | data formatting | bytes 1048576

commit v5 on v3

--- a/solution.py
+++ b/solution.py
@@ -19,6 +19,7 @@
 LANES = 128
 SPAN = 256
 ROWS = 8
+FAN = 2
 HALO = 16
 spread_width = 1.25
 MESH = pl.DeviceIdType.MESH
@@ -122,8 +123,8 @@
     field, energy, refs = refs[0], refs[1], refs[2:]
     held_in, refs = refs[:n_in], refs[n_in:]
     (
-        buf, planes, wz, wx, acc, other, dual, dual_other, pz, t2, field_v, ez, ex,
-        in_sem, zs_sem, zr_sem, xs_sem, xr_sem, ps_sem, pr_sem, es_sem, er_sem, fs_sem, fr_sem, o_sem,
+        buf, planes, wz, wx, acc, from_x, other, dual, dual_other, pz, t2, field_v, ez, ex,
+        in_sem, zs_sem, zr_sem, xs_sem, xr_sem, ps_sem, pr_sem, ns_sem, nr_sem, es_sem, er_sem, fs_sem, fr_sem, o_sem,
     ) = refs
     cx, cy, cz, off, charge, count, amp, dens_v, nodes, factors = held_in[:10]
     down, up = held_in[10 : 10 + LEVELS], held_in[10 + LEVELS :]
@@ -133,6 +134,7 @@
     me = lax.axis_index("slab")
     col = lax.axis_index("blk")
     core = lax.axis_index("sub")
+    beside = 1 - 2 * lax.rem(col, 2)
     wide = 2 * BQ
     fine_y = plan.rows[1]
 
@@ -187,7 +189,7 @@
     def x_copy(p, j):
         return pltpu.make_async_remote_copy(
             src_ref=buf.at[0, j], dst_ref=buf.at[p, j], send_sem=xs_sem.at[p, j], recv_sem=xr_sem.at[p, j],
-            device_id=at(0, -p, 0), device_id_type=MESH,
+            device_id=at(0, -(cols // FAN), 0), device_id_type=MESH,
         )
 
     acc[...] = jnp.zeros_like(acc)
@@ -228,7 +230,7 @@
             jnp.concatenate(split(on_y), axis=0), pz[l, 0:LANES, :], (((1,), (1,)), ((), ())),
             preferred_element_type=jnp.float32,
         )
-        dual[start : start + rows, :] = both[:rows] + both[rows:]
+        dual[0, start : start + rows, :] = both[:rows] + both[rows:]
 
     def swap(k, src, dst):
         return pltpu.make_async_remote_copy(
@@ -236,7 +238,16 @@
             device_id=at(0, 0, 1), device_id_type=MESH,
         )
 
-    swap(0, dual, dual_other).start()
+    def pass_beside(k, src, dst):
+        return pltpu.make_async_remote_copy(
+            src_ref=src, dst_ref=dst, send_sem=ns_sem.at[k], recv_sem=nr_sem.at[k],
+            device_id=at(0, beside, 0), device_id_type=MESH,
+        )
+
+    swap(0, dual.at[0], dual_other).start()
+    swap(0, dual.at[0], dual_other).wait()
+    dual[0] = dual[0] + dual_other[...]
+    pass_beside(0, dual.at[0], dual.at[1]).start()
 
     scale = 2.0**32
     top = 2.0**31 - 128.0
@@ -253,7 +264,7 @@
             lanes = slice(c, c + SPAN)
             chunk = buf[p, j, :, lanes]
             ux = fixed(chunk[1:2, :], G0X) - me * (2**32 // slabs)
-            uy = fixed(chunk[2:3, :], G0Y) - col * (2**32 // cols)
+            uy = fixed(chunk[2:3, :], G0Y)
             uz = fixed(chunk[3:4, :], G0Z)
 
             def squared(first, rows, at_line, factor):
@@ -267,33 +278,37 @@
                         value = jnp.exp2(power if times == 1.0 else power * times).astype(jnp.bfloat16)
                         to = plan.zrow[l] + place * plan.zset + r
                         wz[s, to : to + ROWS, lanes] = value
-            along_y = [[None] * len(ORDER[l]) for l in range(LEVELS)]
-            for i, ((l0, _), uses) in enumerate(SETS):
-                power = squared(plan.ytable + i * plan.yset, plan.yset, uy, exponent(plan.gy[l0]))
-                for l, place, times in uses:
-                    along_y[l][place] = jnp.exp2(power if times == 1.0 else power * times)
             weighted = chunk[0:1, :] * jnp.exp2(squared(0, HALO, ux, broad(factors[0:HALO, :])))
-            last = jnp.exp2(squared(HALO, HALO, uy, broad(factors[HALO : 2 * HALO, :])))
             wx[s, :, lanes] = weighted
-            edge = (weighted * last).astype(jnp.bfloat16)
-            for l in range(LEVELS):
-                start, main, ny = plan.start[l], plan.main[l], plan.ny[l]
-                planes[s, start + main : start + main + HALO, lanes] = edge
-                tiles = [
-                    wx[s, plan.xrow[l] + x : plan.xrow[l] + x + 1, lanes] * on_y
-                    for x in range(plan.nx[l]) for on_y in along_y[l]
-                ]
-                for t, tile in enumerate(tiles):
-                    to = start + t * plan.yset
-                    planes[s, to : to + plan.yset, lanes] = tile.astype(jnp.bfloat16)
+            for r in range(FAN):
+                uy_r = uy - (col + r * beside) * (2**32 // cols)
+                along_y = [[None] * len(ORDER[l]) for l in range(LEVELS)]
+                for i, ((l0, _), uses) in enumerate(SETS):
+                    power = squared(plan.ytable + i * plan.yset, plan.yset, uy_r, exponent(plan.gy[l0]))
+                    for l, place, times in uses:
+                        along_y[l][place] = jnp.exp2(power if times == 1.0 else power * times)
+                last = jnp.exp2(squared(HALO, HALO, uy_r, broad(factors[HALO : 2 * HALO, :])))
+                edge = (weighted * last).astype(jnp.bfloat16)
+                for l in range(LEVELS):
+                    start, main = FAN * plan.start[l] + r * plan.block[l], plan.main[l]
+                    planes[s, start + main : start + main + HALO, lanes] = edge
+                    tiles = [
+                        wx[s, plan.xrow[l] + x : plan.xrow[l] + x + 1, lanes] * on_y
+                        for x in range(plan.nx[l]) for on_y in along_y[l]
+                    ]
+                    for t, tile in enumerate(tiles):
+                        to = start + t * plan.yset
+                        planes[s, to : to + plan.yset, lanes] = tile.astype(jnp.bfloat16)
 
     def gather_in(s):
         for l in range(LEVELS):
             start, rows = plan.start[l], plan.block[l]
-            acc[start : start + rows, 0 : plan.gz[l]] += lax.dot_general(
-                planes[s, start : start + rows, :], wz[s, plan.zrow[l] : plan.zrow[l] + plan.gz[l], :],
+            terms = lax.dot_general(
+                planes[s, FAN * start : FAN * (start + rows), :], wz[s, plan.zrow[l] : plan.zrow[l] + plan.gz[l], :],
                 (((1,), (1,)), ((), ())), preferred_element_type=jnp.float32,
             )
+            for r in range(FAN):
+                acc[r, start : start + rows, 0 : plan.gz[l]] += terms[r * rows : (r + 1) * rows]
 
     def arrive(j):
         pair = half // 2
@@ -312,33 +327,26 @@
         def _():
             z_copy(slot(j, 1), j + pair, 1, -reach).start()
 
-        for p in range(1, cols):
-            x_copy(p, j).start()
+        x_copy(1, j).start()
 
     steps = half // 2
     far = steps // 2
-    turn = far + cols - 1
-    rest = turn + steps - far
-
-    @pl.loop(0, steps * cols)
+
+    @pl.loop(0, steps * FAN)
     def _(t):
-        early, late = t < far, t >= rest
-        own = early | ((t >= turn) & (t < rest))
-        p = jnp.where(own, 0, jnp.where(late, lax.rem(t + (cols - 1) * rest - rest, cols - 1) + 1, t - far + 1))
-        m = jnp.where(early, t, jnp.where(late, lax.div(t + (cols - 1) - rest, cols - 1), jnp.where(own, t - turn + far, 0)))
-
-        @pl.when((t == 0) | (t == turn))
+        side, place = lax.div(t, far), lax.rem(t, far)
+        p, m = lax.rem(side, FAN), lax.div(side, FAN) * far + place
+
+        @pl.when((p == 0) & (place == 0))
         def _():
-            first = jnp.where(t == 0, 0, 2 * far)
-
             @pl.loop(0, 2 * far)
             def _(j):
-                arrive(first + j)
+                arrive(2 * m + j)
 
         @pl.when(p > 0)
         def _():
-            x_copy(p, 2 * m).wait_recv()
-            x_copy(p, 2 * m + 1).wait_recv()
+            x_copy(1, 2 * m).wait_recv()
+            x_copy(1, 2 * m + 1).wait_recv()
 
         gather_in(1)
         weigh(p, 2 * m, 0)
@@ -346,9 +354,9 @@
         weigh(p, 2 * m + 1, 1)
 
     gather_in(1)
-    swap(1, acc, other).start()
-    swap(0, dual, dual_other).wait_recv()
-    ez[0] = jnp.sum(acc[...] * (dual[...] + dual_other[...]), axis=0, keepdims=True)
+    pass_beside(1, acc.at[1], from_x).start()
+    pass_beside(0, dual.at[0], dual.at[1]).wait_recv()
+    ez[0] = jnp.sum(acc[0] * dual[0] + acc[1] * dual[1], axis=0, keepdims=True)
 
     def e_copy(k):
         return pltpu.make_async_remote_copy(
@@ -358,11 +366,14 @@
 
     for k in range(slabs - 1, 0, -1):
         e_copy(k).start()
-    swap(1, acc, other).wait_recv()
+    pass_beside(1, acc.at[1], from_x).wait_recv()
+    acc[0] = acc[0] + from_x[...]
+    swap(1, acc.at[0], other).start()
+    swap(1, acc.at[0], other).wait_recv()
 
     for l in range(LEVELS):
         start, rows = plan.start[l], plan.block[l]
-        cube = acc[start : start + rows, :] + other[start : start + rows, :]
+        cube = acc[0, start : start + rows, :] + other[start : start + rows, :]
         along_z = jnp.dot(jnp.concatenate(split(cube), axis=1), pz[l], preferred_element_type=jnp.float32)
         t2[plan.xrow[l] * fine_y : (plan.xrow[l] + plan.nx[l]) * fine_y, :] = amp[l] * jnp.dot(
             down[l][...], jnp.concatenate(split(along_z), axis=0), preferred_element_type=jnp.float32
@@ -400,11 +411,11 @@
 
     @pl.loop(0, half)
     def _(j):
-        for p in range(1, cols):
-            x_copy(p, j).wait_send()
-
-    swap(0, dual, dual_other).wait_send()
-    swap(1, acc, other).wait_send()
+        x_copy(1, j).wait_send()
+
+    pass_beside(0, dual.at[0], dual.at[1]).wait_send()
+    pass_beside(1, acc.at[1], from_x).wait_send()
+    swap(1, acc.at[0], other).wait_send()
     store.wait()
     for k in range(1, len(others) + 1):
         f_copy(k).wait_recv()
@@ -433,13 +444,14 @@
         out_specs=(anywhere, smem),
         scratch_shapes=[space(o.shape, o.dtype) for space, o in zip(spaces, operands)]
         + [
-            pltpu.VMEM((cols, slabs // 2, 4, 2 * BQ), jnp.float32),
-            pltpu.VMEM((2, plan.total, 2 * BQ), jnp.bfloat16),
+            pltpu.VMEM((FAN, slabs // 2, 4, 2 * BQ), jnp.float32),
+            pltpu.VMEM((2, FAN * plan.total, 2 * BQ), jnp.bfloat16),
             pltpu.VMEM((2, sum(plan.gz), 2 * BQ), jnp.bfloat16),
             pltpu.VMEM((2, HALO, 2 * BQ), jnp.float32),
+            pltpu.VMEM((FAN, plan.total, LANES), jnp.float32),
             pltpu.VMEM((plan.total, LANES), jnp.float32),
             pltpu.VMEM((plan.total, LANES), jnp.float32),
-            pltpu.VMEM((plan.total, LANES), jnp.float32),
+            pltpu.VMEM((FAN, plan.total, LANES), jnp.float32),
             pltpu.VMEM((plan.total, LANES), jnp.float32),
             pltpu.VMEM((LEVELS, 2 * LANES, LANES), jnp.bfloat16),
             pltpu.VMEM((sum(plan.nx) * density.shape[1], LANES), jnp.float32),
@@ -448,7 +460,8 @@
             pltpu.VMEM((2 * cols, 1, LANES), jnp.float32),
             dma((n_in,)),
             dma((slabs // 2, 2)), dma((slabs // 2, 2)),
-            dma((cols, slabs // 2)), dma((cols, slabs // 2)),
+            dma((FAN, slabs // 2)), dma((FAN, slabs // 2)),
+            dma((2,)), dma((2,)),
             dma((2,)), dma((2,)),
             dma((slabs,)), dma((slabs,)),
             dma((2 * cols,)), dma((2 * cols,)),

time: 58.8 us -> 59.2 us (level)
  no operation moved by 1% of the time
where the time goes in v5:
time: 59.2 us; the launch traced here: 59 us
  Pallas kernels  54.1 us (91%)
  between operations  2.98 us (5%)
  local copies, waits for them, and re-layouts  1.89 us (3%)
    pallas_call x1, Pallas kernels, on_device(): pl.pallas_call(functools.partial(kernel, plan, n_in), out_shape=(jax.Shap...  54.1 us
    unnamed x1, local copies, waits for them, and re-layouts  1.89 us

profile of v5, /device:TPU:33, one launch (start us, length us, event | category | flops | bytes accessed | tf_op | source)
XLA Modules:
  0.0 59.0 jit_solution(4413078193712352443)
XLA Ops:
  1.3 54.1 %shard_map.185 = (f32[16,64,128]{2,1,0:T(8,128)}, f32[1,1]{1,0:T(1,128)}) custom-call(s32[1,256]{1,0:T(1,128)} %bitcast.7, s32[1,256]{1,0:T(1,128)} %bitcast.8, s32[1,256]{1,0:T(1,128)} %bitcast.9, f32[3,256]{1,0:T(4,128)} %refs_3_.1, f32[1,256]{1,0:T(1,128)} %bitcast.10, s32[1,1]{1,0:T(1,128)} %bitcast.6.refs_5_, f32[4]{0:T(128)} %refs_6_.1, ...), custom_call_target="tpu_custom_call" | custom-call | tf_op jit(solution)/shard_map/pallas_call | solution.py:440
  55.4 1.9 %copy.23 = f32[16,64,128]{2,1,0:T(8,128)} copy(f32[16,64,128]{2,1,0:T(8,128)} %get-tuple-element.8) | data formatting | bytes 1048576

commit v6 on v5

--- a/solution.py
+++ b/solution.py
@@ -245,9 +245,6 @@
         )
 
     swap(0, dual.at[0], dual_other).start()
-    swap(0, dual.at[0], dual_other).wait()
-    dual[0] = dual[0] + dual_other[...]
-    pass_beside(0, dual.at[0], dual.at[1]).start()
 
     scale = 2.0**32
     top = 2.0**31 - 128.0
@@ -328,6 +325,26 @@
             z_copy(slot(j, 1), j + pair, 1, -reach).start()
 
         x_copy(1, j).start()
+
+        @pl.when(j == 1)
+        def _():
+            swap(0, dual.at[0], dual_other).wait()
+            dual[0] = dual[0] + dual_other[...]
+
+        near_piece = plan.total // pair
+        far_piece = near_piece * (pair - 2) // half
+
+        def piece(first, rows):
+            rows = pl.ds(pl.multiple_of(first, 8), rows)
+            pass_beside(0, dual.at[0, rows, :], dual.at[1, rows, :]).start()
+
+        @pl.when((j > 1) & (j < pair))
+        def _():
+            piece((j - 2) * near_piece, near_piece)
+
+        @pl.when(j >= pair)
+        def _():
+            piece((pair - 2) * near_piece + (j - pair) * 2 * far_piece, 2 * far_piece)
 
     steps = half // 2
     far = steps // 2

time: 59.2 us -> 57.8 us (0.976)
  Pallas kernels: 54.1 us -> 52.7 us
    pallas_call x1, Pallas kernels: 54.1 us -> 52.7 us  [on_device(): pl.pallas_call(functools.partial(kernel, plan, n_in), out_shape=(jax.Shap...]
where the time goes in v6:
time: 57.8 us; the launch traced here: 57.6 us
  Pallas kernels  52.7 us (91%)
  between operations  2.98 us (5%)
  local copies, waits for them, and re-layouts  1.89 us (3%)
    pallas_call x1, Pallas kernels, on_device(): pl.pallas_call(functools.partial(kernel, plan, n_in), out_shape=(jax.Shap...  52.7 us
    unnamed x1, local copies, waits for them, and re-layouts  1.89 us

profile of v6, /device:TPU:33, one launch (start us, length us, event | category | flops | bytes accessed | tf_op | source)
XLA Modules:
  0.0 57.6 jit_solution(11944188128996617428)
XLA Ops:
  1.3 52.7 %shard_map.185 = (f32[16,64,128]{2,1,0:T(8,128)}, f32[1,1]{1,0:T(1,128)}) custom-call(s32[1,256]{1,0:T(1,128)} %bitcast.7, s32[1,256]{1,0:T(1,128)} %bitcast.8, s32[1,256]{1,0:T(1,128)} %bitcast.9, f32[3,256]{1,0:T(4,128)} %refs_3_.1, f32[1,256]{1,0:T(1,128)} %bitcast.10, s32[1,1]{1,0:T(1,128)} %bitcast.6.refs_5_, f32[4]{0:T(128)} %refs_6_.1, ...), custom_call_target="tpu_custom_call" | custom-call | tf_op jit(solution)/shard_map/pallas_call | solution.py:457
  54.0 1.9 %copy.23 = f32[16,64,128]{2,1,0:T(8,128)} copy(f32[16,64,128]{2,1,0:T(8,128)} %get-tuple-element.8) | data formatting | bytes 1048576

commit v7 on v6

--- a/solution.py
+++ b/solution.py
@@ -354,11 +354,13 @@
         side, place = lax.div(t, far), lax.rem(t, far)
         p, m = lax.rem(side, FAN), lax.div(side, FAN) * far + place
 
-        @pl.when((p == 0) & (place == 0))
-        def _():
+        @pl.when((t == 0) | (t == FAN * far - 1))
+        def _():
+            first = jnp.where(t == 0, 0, 2 * far)
+
             @pl.loop(0, 2 * far)
             def _(j):
-                arrive(2 * m + j)
+                arrive(first + j)
 
         @pl.when(p > 0)
         def _():
@@ -386,6 +388,20 @@
     pass_beside(1, acc.at[1], from_x).wait_recv()
     acc[0] = acc[0] + from_x[...]
     swap(1, acc.at[0], other).start()
+    for k in range(1, slabs):
+        e_copy(k).wait_recv()
+    ex[0] = jnp.sum(ez[...], axis=0)
+
+    def f_copy(k):
+        dc, dk = others[k - 1]
+        return pltpu.make_async_remote_copy(
+            src_ref=ex.at[0], dst_ref=ex.at[k], send_sem=fs_sem.at[k], recv_sem=fr_sem.at[k],
+            device_id=at(0, -dc, dk), device_id_type=MESH,
+        )
+
+    for k in range(len(others), 0, -1):
+        f_copy(k).start()
+
     swap(1, acc.at[0], other).wait_recv()
 
     for l in range(LEVELS):
@@ -407,20 +423,6 @@
         field_v[a] = value
     store = pltpu.make_async_copy(field_v, field, o_sem)
     store.start()
-
-    for k in range(1, slabs):
-        e_copy(k).wait_recv()
-    ex[0] = jnp.sum(ez[...], axis=0)
-
-    def f_copy(k):
-        dc, dk = others[k - 1]
-        return pltpu.make_async_remote_copy(
-            src_ref=ex.at[0], dst_ref=ex.at[k], send_sem=fs_sem.at[k], recv_sem=fr_sem.at[k],
-            device_id=at(0, -dc, dk), device_id_type=MESH,
-        )
-
-    for k in range(len(others), 0, -1):
-        f_copy(k).start()
 
     for k in range(1, slabs):
         z_copy(slot(0, 0), k // 2, k % 2, 1).wait_send()

time: 57.8 us -> 56.4 us (0.976)
  Pallas kernels: 52.7 us -> 51.3 us
    pallas_call x1, Pallas kernels: 52.7 us -> 51.3 us  [on_device(): pl.pallas_call(functools.partial(kernel, plan, n_in), out_shape=(jax.Shap...]
where the time goes in v7:
time: 56.4 us; the launch traced here: 56.2 us
  Pallas kernels  51.3 us (91%)
  between operations  2.98 us (5%)
  local copies, waits for them, and re-layouts  1.89 us (3%)
    pallas_call x1, Pallas kernels, on_device(): pl.pallas_call(functools.partial(kernel, plan, n_in), out_shape=(jax.Shap...  51.3 us
    unnamed x1, local copies, waits for them, and re-layouts  1.89 us

profile of v7, /device:TPU:33, one launch (start us, length us, event | category | flops | bytes accessed | tf_op | source)
XLA Modules:
  0.0 56.2 jit_solution(3836278111456188299)
XLA Ops:
  1.3 51.3 %shard_map.185 = (f32[16,64,128]{2,1,0:T(8,128)}, f32[1,1]{1,0:T(1,128)}) custom-call(s32[1,256]{1,0:T(1,128)} %bitcast.7, s32[1,256]{1,0:T(1,128)} %bitcast.8, s32[1,256]{1,0:T(1,128)} %bitcast.9, f32[3,256]{1,0:T(4,128)} %refs_3_.1, f32[1,256]{1,0:T(1,128)} %bitcast.10, s32[1,1]{1,0:T(1,128)} %bitcast.6.refs_5_, f32[4]{0:T(128)} %refs_6_.1, ...), custom_call_target="tpu_custom_call" | custom-call | tf_op jit(solution)/shard_map/pallas_call | solution.py:459
  52.6 1.9 %copy.23 = f32[16,64,128]{2,1,0:T(8,128)} copy(f32[16,64,128]{2,1,0:T(8,128)} %get-tuple-element.8) | data formatting | bytes 1048576

commit v8 on v7

--- a/solution.py
+++ b/solution.py
@@ -124,7 +124,7 @@
     held_in, refs = refs[:n_in], refs[n_in:]
     (
         buf, planes, wz, wx, acc, from_x, other, dual, dual_other, pz, t2, field_v, ez, ex,
-        in_sem, zs_sem, zr_sem, xs_sem, xr_sem, ps_sem, pr_sem, ns_sem, nr_sem, es_sem, er_sem, fs_sem, fr_sem, o_sem,
+        in_sem, zs_sem, zr_sem, ws_sem, wr_sem, xs_sem, xr_sem, ps_sem, pr_sem, ns_sem, nr_sem, es_sem, er_sem, fs_sem, fr_sem, o_sem,
     ) = refs
     cx, cy, cz, off, charge, count, amp, dens_v, nodes, factors = held_in[:10]
     down, up = held_in[10 : 10 + LEVELS], held_in[10 + LEVELS :]
@@ -158,6 +158,8 @@
         pl.semaphore_signal(barrier, inc=1, device_id=at(ds, 0, 0), device_id_type=MESH)
     for dc, dk in others:
         pl.semaphore_signal(barrier, inc=1, device_id=at(0, dc, dk), device_id_type=MESH)
+    for ds in (reach, -reach):
+        pl.semaphore_signal(barrier, inc=1, device_id=at(ds, cols // FAN, 0), device_id_type=MESH)
 
     loads = [pltpu.make_async_copy(hbm[i], held_in[i], in_sem.at[i]) for i in range(n_in)]
     for load in loads:
@@ -172,7 +174,7 @@
     buf[0, 0, 2:3, 0:BQ] = cy[...].astype(jnp.float32) + off[1:2, :]
     buf[0, 0, 3:4, 0:BQ] = cz[...].astype(jnp.float32) + off[2:3, :]
 
-    pl.semaphore_wait(barrier, len(near) + len(others))
+    pl.semaphore_wait(barrier, len(near) + len(others) + 2)
 
     def slot(j, part):
         return buf.at[0, j, :, pl.ds(part * BQ, BQ)]
@@ -183,6 +185,14 @@
             device_id=at(ds, 0, 0), device_id_type=MESH,
         )
 
+    def far_copy(src, j, part, ds):
+        return pltpu.make_async_remote_copy(
+            src_ref=src, dst_ref=buf.at[1, j, :, pl.ds(part * BQ, BQ)],
+            send_sem=ws_sem.at[j, part], recv_sem=wr_sem.at[j, part],
+            device_id=at(ds, -(cols // FAN), 0), device_id_type=MESH,
+        )
+
+    far_copy(slot(0, 0), reach, 0, reach).start()
     for k in range(2 * reach, 0, -1):
         z_copy(slot(0, 0), k // 2, k % 2, -order[k]).start()
 
@@ -319,32 +329,32 @@
         @pl.when((j > 0) & (j < pair))
         def _():
             z_copy(slot(j, 0), j + pair, 0, reach).start()
+            far_copy(slot(j, 0), j + pair, 0, reach).start()
 
         @pl.when(j < pair)
         def _():
             z_copy(slot(j, 1), j + pair, 1, -reach).start()
-
-        x_copy(1, j).start()
+            far_copy(slot(j, 1), j + pair, 1, -reach).start()
+            x_copy(1, j).start()
 
         @pl.when(j == 1)
         def _():
             swap(0, dual.at[0], dual_other).wait()
             dual[0] = dual[0] + dual_other[...]
 
-        near_piece = plan.total // pair
-        far_piece = near_piece * (pair - 2) // half
-
         def piece(first, rows):
-            rows = pl.ds(pl.multiple_of(first, 8), rows)
+            rows = pl.ds(first, rows)
             pass_beside(0, dual.at[0, rows, :], dual.at[1, rows, :]).start()
 
-        @pl.when((j > 1) & (j < pair))
-        def _():
-            piece((j - 2) * near_piece, near_piece)
-
-        @pl.when(j >= pair)
-        def _():
-            piece((pair - 2) * near_piece + (j - pair) * 2 * far_piece, 2 * far_piece)
+        quarter = plan.total // 4
+
+        @pl.when(j == pair - 2)
+        def _():
+            piece(0, quarter)
+
+        @pl.when(j == pair - 1)
+        def _():
+            piece(quarter, 3 * quarter)
 
     steps = half // 2
     far = steps // 2
@@ -354,7 +364,7 @@
         side, place = lax.div(t, far), lax.rem(t, far)
         p, m = lax.rem(side, FAN), lax.div(side, FAN) * far + place
 
-        @pl.when((t == 0) | (t == FAN * far - 1))
+        @pl.when((t == 0) | (t == FAN * far))
         def _():
             first = jnp.where(t == 0, 0, 2 * far)
 
@@ -362,10 +372,16 @@
             def _(j):
                 arrive(first + j)
 
-        @pl.when(p > 0)
+        @pl.when((p > 0) & (m < far))
         def _():
             x_copy(1, 2 * m).wait_recv()
             x_copy(1, 2 * m + 1).wait_recv()
+
+        @pl.when((p > 0) & (m >= far))
+        def _():
+            for i in range(2):
+                for part in range(2):
+                    far_copy(slot(0, 0), 2 * m + i, part, reach).wait_recv()
 
         gather_in(1)
         weigh(p, 2 * m, 0)
@@ -428,9 +444,11 @@
         z_copy(slot(0, 0), k // 2, k % 2, 1).wait_send()
         e_copy(k).wait_send()
 
-    @pl.loop(0, half)
+    @pl.loop(0, reach)
     def _(j):
         x_copy(1, j).wait_send()
+        for part in range(2):
+            far_copy(slot(0, 0), j + reach, part, reach).wait_send()
 
     pass_beside(0, dual.at[0], dual.at[1]).wait_send()
     pass_beside(1, acc.at[1], from_x).wait_send()
@@ -479,6 +497,7 @@
             pltpu.VMEM((2 * cols, 1, LANES), jnp.float32),
             dma((n_in,)),
             dma((slabs // 2, 2)), dma((slabs // 2, 2)),
+            dma((slabs // 2, 2)), dma((slabs // 2, 2)),
             dma((FAN, slabs // 2)), dma((FAN, slabs // 2)),
             dma((2,)), dma((2,)),
             dma((2,)), dma((2,)),

time: 56.4 us -> 58.3 us (1.034)
  Pallas kernels: 51.3 us -> 53.2 us
    pallas_call x1, Pallas kernels: 51.3 us -> 53.2 us  [on_device(): pl.pallas_call(functools.partial(kernel, plan, n_in), out_shape=(jax.Shap...]
where the time goes in v8:
time: 58.3 us; the launch traced here: 58.1 us
  Pallas kernels  53.2 us (91%)
  between operations  2.98 us (5%)
  local copies, waits for them, and re-layouts  1.89 us (3%)
    pallas_call x1, Pallas kernels, on_device(): pl.pallas_call(functools.partial(kernel, plan, n_in), out_shape=(jax.Shap...  53.2 us
    unnamed x1, local copies, waits for them, and re-layouts  1.89 us

profile of v8, /device:TPU:33, one launch (start us, length us, event | category | flops | bytes accessed | tf_op | source)
XLA Modules:
  0.0 58.1 jit_solution(7342874976780227096)
XLA Ops:
  1.3 53.2 %shard_map.185 = (f32[16,64,128]{2,1,0:T(8,128)}, f32[1,1]{1,0:T(1,128)}) custom-call(s32[1,256]{1,0:T(1,128)} %bitcast.7, s32[1,256]{1,0:T(1,128)} %bitcast.8, s32[1,256]{1,0:T(1,128)} %bitcast.9, f32[3,256]{1,0:T(4,128)} %refs_3_.1, f32[1,256]{1,0:T(1,128)} %bitcast.10, s32[1,1]{1,0:T(1,128)} %bitcast.6.refs_5_, f32[4]{0:T(128)} %refs_6_.1, ...), custom_call_target="tpu_custom_call" | custom-call | tf_op jit(solution)/shard_map/pallas_call | solution.py:477
  54.5 1.9 %copy.23 = f32[16,64,128]{2,1,0:T(8,128)} copy(f32[16,64,128]{2,1,0:T(8,128)} %get-tuple-element.8) | data formatting | bytes 1048576

commit v9 on v7

--- a/solution.py
+++ b/solution.py
@@ -331,20 +331,9 @@
             swap(0, dual.at[0], dual_other).wait()
             dual[0] = dual[0] + dual_other[...]
 
-        near_piece = plan.total // pair
-        far_piece = near_piece * (pair - 2) // half
-
-        def piece(first, rows):
-            rows = pl.ds(pl.multiple_of(first, 8), rows)
-            pass_beside(0, dual.at[0, rows, :], dual.at[1, rows, :]).start()
-
-        @pl.when((j > 1) & (j < pair))
-        def _():
-            piece((j - 2) * near_piece, near_piece)
-
-        @pl.when(j >= pair)
-        def _():
-            piece((pair - 2) * near_piece + (j - pair) * 2 * far_piece, 2 * far_piece)
+        @pl.when(j == pair - 1)
+        def _():
+            pass_beside(0, dual.at[0], dual.at[1]).start()
 
     steps = half // 2
     far = steps // 2

time: 56.4 us -> 56.3 us (level)
  no operation moved by 1% of the time
where the time goes in v9:
time: 56.3 us; the launch traced here: 56.1 us
  Pallas kernels  51.3 us (91%)
  between operations  2.98 us (5%)
  local copies, waits for them, and re-layouts  1.89 us (3%)
    pallas_call x1, Pallas kernels, on_device(): pl.pallas_call(functools.partial(kernel, plan, n_in), out_shape=(jax.Shap...  51.3 us
    unnamed x1, local copies, waits for them, and re-layouts  1.89 us

profile of v9, /device:TPU:33, one launch (start us, length us, event | category | flops | bytes accessed | tf_op | source)
XLA Modules:
  0.0 56.1 jit_solution(16043943866361181177)
XLA Ops:
  1.3 51.3 %shard_map.185 = (f32[16,64,128]{2,1,0:T(8,128)}, f32[1,1]{1,0:T(1,128)}) custom-call(s32[1,256]{1,0:T(1,128)} %bitcast.7, s32[1,256]{1,0:T(1,128)} %bitcast.8, s32[1,256]{1,0:T(1,128)} %bitcast.9, f32[3,256]{1,0:T(4,128)} %refs_3_.1, f32[1,256]{1,0:T(1,128)} %bitcast.10, s32[1,1]{1,0:T(1,128)} %bitcast.6.refs_5_, f32[4]{0:T(128)} %refs_6_.1, ...), custom_call_target="tpu_custom_call" | custom-call | tf_op jit(solution)/shard_map/pallas_call | solution.py:448
  52.5 1.9 %copy.23 = f32[16,64,128]{2,1,0:T(8,128)} copy(f32[16,64,128]{2,1,0:T(8,128)} %get-tuple-element.8) | data formatting | bytes 1048576
